TPU v7x, 32 devices: a whole 2x2x4 slice. The times are simulated.
32 devices in a mesh: seq: 8 (over z, x), head: 4 (over y, core).
Axes of the slice: x: 2, y: 2, z: 4, core: 2. Of those that a mesh axis runs over, the one named last changes fastest.
Arguments:
- inputs: bfloat16 [24, 1024, 512], P('seq', 'head'), may hold values from -6 to 6
- cotangent: bfloat16 [24, 1024, 512], P('seq', 'head'), may hold values from -6 to 6
- span_offset: int32 [24, 64], P('seq', 'head'), may hold values from 0 to 8
- span_len: int32 [24, 64], P('seq', 'head'), may hold values from 1 to 8
- owner_slot: int32 [256], replicated, may hold values from 0 to 255, as said below
- master: float32 [256, 128, 128], P(('seq', 'head')), as said below
- moment_one: float32 [256, 128, 128], P(('seq', 'head')), as said below
- moment_two: float32 [256, 128, 128], P(('seq', 'head')), may hold values from 294.912 to 29491.2, as said below
- basis_left: float32 [256, 128, 128], P(('seq', 'head')), may hold values from -1 to 1, as said below
- basis_right: float32 [256, 128, 128], P(('seq', 'head')), may hold values from -1 to 1, as said below
- average: float32 [256, 128, 128], P(('seq', 'head')), may hold values from -0.25 to 0.25
- vec_master: float32 [6144], P(('seq', 'head')), as said below
- vec_moment_one: float32 [6144], P(('seq', 'head')), may hold values from -343.46005 to 343.46005
- vec_moment_two: float32 [6144], P(('seq', 'head')), may hold values from 7372.8 to 29491.2
Outputs:
- layer_out: bfloat16 [24, 1024, 512], P('seq', 'head')
- input_grad: float32 [24, 1024, 512], P('seq', 'head')
- slot_grad: float32 [256, 128, 128], P(('seq', 'head'))
- vec_grad: float32 [6144], P(('seq', 'head'))
- new_moment_one: float32 [256, 128, 128], P(('seq', 'head'))
- new_moment_two: float32 [256, 128, 128], P(('seq', 'head'))
- new_master: float32 [256, 128, 128], P(('seq', 'head'))
- new_master_bf16: bfloat16 [256, 128, 128], P(('seq', 'head'))
- new_average: float32 [256, 128, 128], P(('seq', 'head'))
- new_vec_moment_one: float32 [6144], P(('seq', 'head'))
- new_vec_moment_two: float32 [6144], P(('seq', 'head'))
- new_vec: float32 [6144], P(('seq', 'head'))
Inputs may be any that keep to these rules, and one draw needn't show every extreme that they name: `owner_slot`: A permutation of the slots; values of 192 or more mark empty slots. `master`: Real-valued blocks. `moment_one`: Real-valued, of both signs. `moment_two`: Positive. `basis_left`: each block is orthogonal. `basis_right`: each block is orthogonal. `vec_master`: the gains g_1 and g_2 are positive.
All inputs are finite; a program needn't handle non-finite values.
Results may differ from a plain program's by a relative error of at most 0.013.
The roundings to bfloat16 on the way count: a program that leaves them out, or rounds other values in their place, can miss the bound.
Values may be sent and summed in bfloat16 or wider, within the bound.
A program may use at most 128 MiB of HBM per device.

v0:
```python
import functools
import math

import jax
import jax.numpy as jnp
from jax import lax
from jax.experimental import pallas as pl
from jax.experimental.pallas import tpu as pltpu
from jax.sharding import PartitionSpec as P

D = 512
FF = 2048
WIN = 16
BLK = 128
STEP = 5
HD = 64
NBLK = 192
QUERIES = 256
SCALE = 1.0 / math.sqrt(HD)


NORM_EPS = 1e-06
ADAM_EPS = 1e-08
RATE = 0.05
VEC_RATE = 0.2
DECAY = 0.01
KEEP = 0.9
HIGH = lax.Precision.HIGHEST


def split_vector(vector):
    widths = [D, D, D, D, D, FF, D, D, D]
    pieces = []
    offset = 0
    for extent in widths:
        pieces.append(vector[offset : offset + extent])
        offset = offset + extent
    return pieces


def layer_norm(values, gain, shift):
    center = values - jnp.mean(values, axis=-1, keepdims=True)
    spread = jnp.mean(center * center, axis=-1, keepdims=True)
    return center * lax.rsqrt(spread + NORM_EPS) * gain + shift


def gelu_value(values):
    return 0.5 * values * (1.0 + lax.erf(values * 0.7071067811865476))


def gelu_slope(values):
    return (
        0.5 * (1.0 + lax.erf(values * 0.7071067811865476))
        + values * jnp.exp(-0.5 * values * values) * 0.3989422804014327
    )


def span_mask(span_offset, span_len):
    offsets = jnp.repeat(span_offset, WIN, axis=1)
    extents = jnp.repeat(span_len, WIN, axis=1)
    within = (jnp.arange(offsets.shape[1], dtype=jnp.int32) % WIN)[None, :]
    return ((within >= offsets) & (within < offsets + extents)).astype(jnp.float32)


def contract(left, right, left_axis, right_axis):
    return lax.dot_general(
        left, right, (((left_axis,), (right_axis,)), ((), ())), preferred_element_type=jnp.float32
    )


def swap(source, target, send_sem, recv_sem, own_sem, item):
    head_size = source.shape[1]
    seq = lax.axis_index("seq")
    head = lax.axis_index("head")
    copies = []
    for step in [2, 1, 3] if head_size == 4 else range(1, head_size):
        peer = lax.rem(head + step, head_size)
        copies.append(
            pltpu.make_async_remote_copy(
                src_ref=source.at[item, peer],
                dst_ref=target.at[head, item],
                send_sem=send_sem.at[item, step],
                recv_sem=recv_sem.at[item, step],
                device_id=(seq, peer),
                device_id_type=MESH,
            )
        )
    copies.append(
        pltpu.make_async_copy(source.at[item, head], target.at[head, item], own_sem.at[item])
    )
    return copies


def swap_step(source, target, send_sem, recv_sem, own_sem):
    item = pl.program_id(0)
    for copy in swap(source, target, send_sem, recv_sem, own_sem, item):
        copy.start()

    @pl.when(item == pl.num_programs(0) - 1)
    def _():
        for number in range(source.shape[0]):
            for copy in swap(source, target, send_sem, recv_sem, own_sem, number):
                copy.wait()


def swap_scratch(items, head_size, tokens, columns):
    return [
        pltpu.VMEM((items, head_size, tokens, columns), jnp.bfloat16),
        pltpu.SemaphoreType.DMA((items, head_size)),
        pltpu.SemaphoreType.DMA((items, head_size)),
        pltpu.SemaphoreType.DMA((items,)),
    ]


def forward_kernel(
    x_ref, w_ref, b_ref, qkv_ref, ctx_out, lse_ref, ctx_ref, send_sem, recv_sem, own_sem
):
    item = pl.program_id(0)

    @pl.when(item == 0)
    def _():
        greet_head(ctx_ref.shape[1])

    head_size, tokens, width = x_ref.shape[0], x_ref.shape[1], x_ref.shape[2]
    length = head_size * tokens
    cols = w_ref.shape[1] // 3
    rows = x_ref[...].reshape(length, width)
    qkv_ref[...] = (contract(rows, w_ref[...], 1, 0) + b_ref[...]).astype(jnp.bfloat16)
    step = min(QUERIES, tokens)
    for number in range(cols // HD):
        low = number * HD
        keys = qkv_ref[:, cols + low : cols + low + HD]
        values = qkv_ref[:, 2 * cols + low : 2 * cols + low + HD]
        for begin in range(0, length, step):
            query = qkv_ref[begin : begin + step, low : low + HD] * jnp.bfloat16(SCALE)
            scores = contract(keys, query, 1, 1)
            highest = jnp.max(scores, axis=0, keepdims=True)
            weights = jnp.exp(scores - highest)
            summed = jnp.sum(weights, axis=0, keepdims=True)
            probs = (weights * (1.0 / summed)).astype(jnp.bfloat16)
            context = contract(values, probs, 0, 0).T.astype(jnp.bfloat16)
            ctx_ref[item, begin // tokens, pl.ds(begin % tokens, step), low : low + HD] = context
            lse_ref[number : number + 1, begin : begin + step] = highest + jnp.log(summed)
    swap_step(ctx_ref, ctx_out, send_sem, recv_sem, own_sem)


def attend(inputs_full, weights, bias):
    seq_local, head_size, tokens, width = inputs_full.shape
    length = head_size * tokens
    cols = weights.shape[1] // 3
    return pl.pallas_call(
        forward_kernel,
        grid=(seq_local,),
        out_shape=(
            jax.ShapeDtypeStruct((seq_local, length, 3 * cols), jnp.bfloat16),
            jax.ShapeDtypeStruct((head_size, seq_local, tokens, cols), jnp.bfloat16),
            jax.ShapeDtypeStruct((seq_local, 8, length), jnp.float32),
        ),
        in_specs=[
            pl.BlockSpec((None, head_size, tokens, width), lambda s: (s, 0, 0, 0)),
            pl.BlockSpec((width, 3 * cols), lambda s: (0, 0)),
            pl.BlockSpec((1, 3 * cols), lambda s: (0, 0)),
        ],
        out_specs=(
            pl.BlockSpec((None, length, 3 * cols), lambda s: (s, 0, 0)),
            pl.BlockSpec(memory_space=pl.ANY),
            pl.BlockSpec((None, 8, length), lambda s: (s, 0, 0)),
        ),
        scratch_shapes=swap_scratch(seq_local, head_size, tokens, cols),
        compiler_params=pltpu.CompilerParams(
            collective_id=2, has_side_effects=True, vmem_limit_bytes=48 * 1024 * 1024
        ),
        name="attend",
    )(inputs_full, weights, bias)


def backward_kernel(
    da_ref,
    wo_ref,
    w_ref,
    lse_ref,
    dz_ref,
    df_ref,
    yb_ref,
    ctx_ref,
    h_any,
    du_any,
    x_any,
    qkv_any,
    blocks_ref,
    db_ref,
    grad_ref,
    h_ref,
    du_ref,
    x_ref,
    qkv_ref,
    load_sem,
    dall,
    acc,
    dw_ref,
    dctx_src,
    dctx_send,
    dctx_recv,
    dctx_own,
    d_src,
    d_send,
    d_recv,
    d_own,
    dctx_got,
    d_got,
):
    loads = [
        pltpu.make_async_copy(source, target, load_sem.at[number])
        for number, (source, target) in enumerate(
            [(h_any, h_ref), (du_any, du_ref), (qkv_any, qkv_ref), (x_any, x_ref)]
        )
    ]
    for load in loads:
        load.start()
    head_size, items, tokens, cols = ctx_ref.shape
    width = yb_ref.shape[1]
    hidden = h_ref.shape[1]
    length = head_size * tokens
    across = width // BLK
    greet_head(head_size)

    def dctx_swap(item):
        return swap(dctx_src, dctx_got, dctx_send, dctx_recv, dctx_own, item)

    def d_swap(item):
        return swap(d_src, d_got, d_send, d_recv, d_own, item)

    for item in range(items):
        dctx = contract(da_ref[item * tokens : (item + 1) * tokens], wo_ref[...], 1, 1)
        for head in range(head_size):
            dctx_src[item, head] = dctx[:, head * cols : (head + 1) * cols].astype(jnp.bfloat16)
        for copy in dctx_swap(item):
            copy.start()

    first = 3 * across * across
    for head in range(head_size):
        value = contract(ctx_ref[head].reshape(items * tokens, cols), da_ref[...], 0, 0)
        value = value.astype(jnp.bfloat16)
        for begin in range(0, cols, min(cols, BLK)):
            row = head * cols + begin
            part = min(cols, BLK)
            for col in range(across):
                number = first + (row // BLK) * across + col
                blocks_ref[number, row % BLK : row % BLK + part] = value[
                    begin : begin + part, col * BLK : (col + 1) * BLK
                ]
    first = 4 * across * across
    wide = hidden // BLK
    loads[1].wait()

    def up_part(turn, carry):
        span = pl.ds(pl.multiple_of(turn * width, width), width)
        value = contract(yb_ref[...], du_ref[:, span], 0, 0).astype(jnp.bfloat16)
        for row in range(across):
            for col in range(across):
                blocks_ref[first + row * wide + turn * across + col] = value[
                    row * BLK : (row + 1) * BLK, col * BLK : (col + 1) * BLK
                ]
        return carry

    lax.fori_loop(0, hidden // width, up_part, 0)
    loads[0].wait()
    second = first + across * wide

    def down_part(turn, carry):
        span = pl.ds(pl.multiple_of(turn * width, width), width)
        value = contract(h_ref[:, span], df_ref[...], 0, 0).astype(jnp.bfloat16)
        for row in range(across):
            for col in range(across):
                blocks_ref[second + (turn * across + row) * across + col] = value[
                    row * BLK : (row + 1) * BLK, col * BLK : (col + 1) * BLK
                ]
        return carry

    lax.fori_loop(0, hidden // width, down_part, 0)
    dw_ref[...] = jnp.zeros_like(dw_ref)
    db_ref[...] = jnp.zeros_like(db_ref)
    loads[2].wait()
    loads[3].wait()
    step = min(QUERIES, tokens)
    scale = jnp.bfloat16(SCALE)

    def attend_item(item, carry):
        for copy in dctx_swap(item):
            copy.wait()
        for number in range(cols // HD):
            low = number * HD
            keys = qkv_ref[item, :, cols + low : cols + low + HD]
            values = qkv_ref[item, :, 2 * cols + low : 2 * cols + low + HD]
            for begin in range(0, length, step):
                query = qkv_ref[item, begin : begin + step, low : low + HD] * scale
                dctx = dctx_got[
                    begin // tokens, item, pl.ds(begin % tokens, step), low : low + HD
                ]
                scores = contract(keys, query, 1, 1)
                probs = jnp.exp(scores - lse_ref[item, number : number + 1, begin : begin + step])
                dprobs = contract(values, dctx, 1, 1)
                inner = jnp.sum(probs * dprobs, axis=0, keepdims=True)
                dscores = (probs * (dprobs - inner)).astype(jnp.bfloat16)
                dkey = contract(dscores, query, 1, 0)
                dvalue = contract(probs.astype(jnp.bfloat16), dctx, 1, 0)
                if begin == 0:
                    acc[0] = dkey
                    acc[1] = dvalue
                else:
                    acc[0] += dkey
                    acc[1] += dvalue
                dquery = contract(keys, dscores, 0, 0).T * SCALE
                dall[begin : begin + step, low : low + HD] = dquery.astype(jnp.bfloat16)
            dall[:, cols + low : cols + low + HD] = acc[0].astype(jnp.bfloat16)
            dall[:, 2 * cols + low : 2 * cols + low + HD] = acc[1].astype(jnp.bfloat16)
        delta = dall[...]
        d_src[item] = delta.reshape(head_size, tokens, 3 * cols)
        for copy in d_swap(item):
            copy.start()
        dw_ref[...] += contract(x_ref[item].reshape(length, width), delta, 0, 0)
        db_ref[...] += jnp.sum(delta.astype(jnp.float32), axis=0, keepdims=True)
        return carry

    lax.fori_loop(0, items, attend_item, 0)

    head_me = lax.axis_index("head")
    for number in range(3):
        value = dw_ref[:, number * cols : (number + 1) * cols].astype(jnp.bfloat16)
        for row in range(across):
            for col in range(across):
                rows = value[row * BLK : (row + 1) * BLK]
                parts = []
                for begin in range(0, BLK, min(cols, BLK)):
                    lane = col * BLK + begin
                    begin_own = lane % cols
                    part = rows[:, begin_own : begin_own + min(cols, BLK)]
                    parts.append(jnp.where(head_me == lane // cols, part, jnp.zeros_like(part)))
                whole = parts[0] if len(parts) == 1 else jnp.concatenate(parts, 1)
                blocks_ref[number * across * across + row * across + col] = whole

    def input_item(item, carry):
        for copy in d_swap(item):
            copy.wait()
        span = pl.ds(pl.multiple_of(item * tokens, tokens), tokens)
        total = dz_ref[span]
        for head in range(head_size):
            total = total + contract(d_got[head, item], w_ref[head], 1, 1)
        grad_ref[item] = total
        return carry

    lax.fori_loop(0, items, input_item, 0)


def backward(d_branch, w_out, w_qkv, lse, d_zone, d_ffn, first_low, context, hidden, d_hidden, inputs_full, qkv):
    head_size, seq_local, tokens, cols = context.shape
    width = w_out.shape[0]
    length = head_size * tokens
    whole = pl.BlockSpec(memory_space=pltpu.VMEM)
    any_space = pl.BlockSpec(memory_space=pl.ANY)

    def like(array):
        return pltpu.VMEM(array.shape, array.dtype)

    return pl.pallas_call(
        backward_kernel,
        out_shape=(
            jax.ShapeDtypeStruct((NBLK, BLK, BLK), jnp.bfloat16),
            jax.ShapeDtypeStruct((1, 3 * cols), jnp.float32),
            jax.ShapeDtypeStruct((seq_local, tokens, width), jnp.float32),
        ),
        in_specs=[whole] * 8 + [any_space] * 4,
        out_specs=(whole, whole, whole),
        scratch_shapes=[
            like(hidden),
            like(d_hidden),
            like(inputs_full),
            like(qkv),
            pltpu.SemaphoreType.DMA((4,)),
            pltpu.VMEM((length, 3 * cols), jnp.bfloat16),
            pltpu.VMEM((2, length, HD), jnp.float32),
            pltpu.VMEM((width, 3 * cols), jnp.float32),
        ]
        + swap_scratch(seq_local, head_size, tokens, cols)
        + swap_scratch(seq_local, head_size, tokens, 3 * cols)
        + [
            pltpu.VMEM((head_size, seq_local, tokens, cols), jnp.bfloat16),
            pltpu.VMEM((head_size, seq_local, tokens, 3 * cols), jnp.bfloat16),
        ],
        compiler_params=pltpu.CompilerParams(
            collective_id=4, has_side_effects=True, vmem_limit_bytes=60 * 1024 * 1024
        ),
        name="backward",
    )(
        d_branch,
        w_out,
        w_qkv,
        lse,
        d_zone,
        d_ffn,
        first_low,
        context,
        hidden,
        d_hidden,
        inputs_full,
        qkv,
    )


def rotate_adam(grads, master, moment_one, moment_two, basis_left, basis_right):
    rotated = jnp.einsum("sji,sjk->sik", basis_left, grads, precision=HIGH)
    rotated = jnp.einsum("sik,skl->sil", rotated, basis_right, precision=HIGH)
    first = 0.5 * moment_one + 0.5 * rotated
    second = 0.5 * moment_two + 0.5 * rotated * rotated
    correct = 1.0 - 0.5**STEP
    normed = first / correct / (jnp.sqrt(second / correct) + ADAM_EPS)
    turned = jnp.einsum("sij,sjk->sik", basis_left, normed, precision=HIGH)
    turned = jnp.einsum("sik,slk->sil", turned, basis_right, precision=HIGH)
    updated = master - RATE * (turned + DECAY * master)
    return (first, second, updated)


def back_product(grads, weight):
    return jnp.einsum("to,io->ti", grads, weight, preferred_element_type=jnp.float32)


MESH = pl.DeviceIdType.MESH
VEC_ROWS = 16
PIECE = 16


def cut(seq_size, head_size):
    cores = 2 if head_size % 2 == 0 else 1
    rows = 1
    while 2 * (rows * 2) ** 2 <= seq_size and seq_size % (rows * 2) == 0:
        rows = rows * 2
    return (seq_size // rows, rows, head_size // cores, cores)


def place(dims):
    size_z, size_x, size_y, size_c = dims
    seq = lax.axis_index("seq")
    head = lax.axis_index("head")
    return (
        lax.div(seq, size_x),
        lax.rem(seq, size_x),
        lax.div(head, size_c),
        lax.rem(head, size_c),
    )


def device(dims, coords):
    return (coords[0] * dims[1] + coords[1], coords[2] * dims[3] + coords[3])


def flat(dims, coords):
    return ((coords[0] * dims[1] + coords[1]) * dims[2] + coords[2]) * dims[3] + coords[3]


def moved(dims, coords, axis, step):
    new = list(coords)
    new[axis] = lax.rem(coords[axis] + step, dims[axis])
    return tuple(new)


def greet(dims, coords):
    barrier = pltpu.get_barrier_semaphore()
    count = 0
    for axis in range(4):
        for step in range(1, dims[axis]):
            pl.semaphore_signal(
                barrier,
                inc=1,
                device_id=device(dims, moved(dims, coords, axis, step)),
                device_id_type=MESH,
            )
            count = count + 1
    pl.semaphore_wait(barrier, count)


def greet_head(head_size):
    barrier = pltpu.get_barrier_semaphore()
    seq = lax.axis_index("seq")
    head = lax.axis_index("head")
    for step in range(1, head_size):
        pl.semaphore_signal(
            barrier, inc=1, device_id=(seq, lax.rem(head + step, head_size)), device_id_type=MESH
        )
    pl.semaphore_wait(barrier, head_size - 1)


def gather_kernel(
    dims,
    inv_ref,
    x_ref,
    w_ref,
    xf_ref,
    qkv_ref,
    out_ref,
    up_ref,
    down_ref,
    vec_ref,
    wf_ref,
    own_sem,
    x_send,
    x_recv,
    w_send,
    w_recv,
):
    me = place(dims)
    size_z, size_x, size_y, size_c = dims
    head_me = me[2] * size_c + me[3]
    chunk = w_ref.shape[0]

    def spot(index):
        return wf_ref.at[pl.ds(index * chunk, chunk)]

    own_x = pltpu.make_async_copy(x_ref, xf_ref.at[:, head_me], own_sem.at[0])
    own_w = pltpu.make_async_copy(w_ref, spot(flat(dims, me)), own_sem.at[1])
    own_x.start()
    own_w.start()
    greet(dims, me)
    started = []

    def send_x(source, head, target, number):
        copy = pltpu.make_async_remote_copy(
            src_ref=source,
            dst_ref=xf_ref.at[:, head],
            send_sem=x_send.at[number],
            recv_sem=x_recv.at[head],
            device_id=device(dims, target),
            device_id_type=MESH,
        )
        copy.start()
        started.append(copy)

    def arrived_x(head):
        pltpu.make_async_remote_copy(
            src_ref=x_ref,
            dst_ref=xf_ref.at[:, head],
            send_sem=x_send.at[0],
            recv_sem=x_recv.at[head],
            device_id=device(dims, me),
            device_id_type=MESH,
        ).wait_recv()

    count = [0]

    def send_w(source, index, target):
        number = count[0]
        count[0] = number + 1
        copy = pltpu.make_async_remote_copy(
            src_ref=source,
            dst_ref=spot(index),
            send_sem=w_send.at[number],
            recv_sem=w_recv.at[index],
            device_id=device(dims, target),
            device_id_type=MESH,
        )
        copy.start()
        started.append(copy)

    def arrived_w(index):
        pltpu.make_async_remote_copy(
            src_ref=w_ref,
            dst_ref=spot(index),
            send_sem=w_send.at[0],
            recv_sem=w_recv.at[index],
            device_id=device(dims, me),
            device_id_type=MESH,
        ).wait_recv()

    order = [0, 2, 1, 3]

    def forward(source, coords, after):
        for axis in order[after:]:
            for step in range(1, dims[axis]):
                send_w(source, flat(dims, coords), moved(dims, me, axis, step))

    number = 0
    for step in range(1, size_y):
        send_x(x_ref, head_me, moved(dims, me, 2, step), number)
        number = number + 1
    for step in range(1, size_c):
        send_x(x_ref, head_me, moved(dims, me, 3, step), number)
        number = number + 1
    forward(w_ref, me, 0)
    held = [me]
    for level in range(3):
        axis = order[level]
        fresh = []
        for step in range(1, dims[axis]):
            for coords in held:
                source = moved(dims, coords, axis, step)
                arrived_w(flat(dims, source))
                forward(spot(flat(dims, source)), source, level + 1)
                fresh.append(source)
        held = held + fresh
        if level == 1:
            for step in range(1, size_y):
                other = moved(dims, me, 2, step)
                head = other[2] * size_c + other[3]
                arrived_x(head)
                for hop in range(1, size_c):
                    send_x(xf_ref.at[:, head], head, moved(dims, me, 3, hop), number)
                    number = number + 1
    for step in range(1, size_c):
        for coords in held:
            arrived_w(flat(dims, moved(dims, coords, 3, step)))
        for across in range(size_y):
            other = moved(dims, moved(dims, me, 3, step), 2, across)
            arrived_x(other[2] * size_c + other[3])
    for copy in started:
        copy.wait_send()
    own_x.wait()
    own_w.wait()
    unpack(dims, inv_ref, wf_ref, qkv_ref, out_ref, up_ref, down_ref)
    chunk = w_ref.shape[0]
    for number in range(vec_ref.shape[0]):
        vec_ref[number] = wf_ref[(number + 1) * chunk - 1]


def unpack(dims, inv_ref, wf_ref, qkv_ref, out_ref, up_ref, down_ref):
    head_size = dims[2] * dims[3]
    width = out_ref.shape[0]
    hidden = up_ref.shape[1]
    cols = width // head_size
    across = width // BLK

    def block(number):
        piece = inv_ref[number]
        return jnp.concatenate([wf_ref[piece + part] for part in range(BLK // PIECE)], 0)

    def rows_of(row_count, first, col_count, store):
        def one(row, carry):
            span = pl.ds(pl.multiple_of(row * BLK, BLK), BLK)
            for col in range(col_count):
                store(span, col, block(first + row * col_count + col))
            return carry

        lax.fori_loop(0, row_count, one, 0)

    for number in range(3):

        def store_qkv(span, col, value, number=number):
            for begin in range(0, BLK, min(cols, BLK)):
                head = (col * BLK + begin) // cols
                lane = (col * BLK + begin) % cols
                part = min(cols, BLK)
                qkv_ref[head, span, number * cols + lane : number * cols + lane + part] = value[
                    :, begin : begin + part
                ]

        rows_of(across, number * across * across, across, store_qkv)

    def store_in(ref):
        def store(span, col, value):
            ref[span, col * BLK : (col + 1) * BLK] = value

        return store

    rows_of(across, 3 * across * across, across, store_in(out_ref))
    first = 4 * across * across
    rows_of(across, first, hidden // BLK, store_in(up_ref))
    first = first + across * (hidden // BLK)
    rows_of(hidden // BLK, first, across, store_in(down_ref))


def gather_all(dims, inverse, inputs, packed):
    size_z, size_x, size_y, size_c = dims
    total = size_z * size_x * size_y * size_c
    head_size = size_y * size_c
    seq_local, tok_local, width = inputs.shape
    any_space = pl.BlockSpec(memory_space=pl.ANY)
    whole = pl.BlockSpec(memory_space=pltpu.VMEM)
    sends_x = (size_y - 1) * size_c + size_c - 1
    sends_w = (
        (size_z - 1)
        + size_z * (size_y - 1)
        + size_z * size_y * (size_x - 1)
        + size_z * size_y * size_x * (size_c - 1)
    )
    return pl.pallas_call(
        functools.partial(gather_kernel, dims),
        out_shape=(
            jax.ShapeDtypeStruct((seq_local, head_size, tok_local, width), inputs.dtype),
            jax.ShapeDtypeStruct((head_size, width, 3 * width // head_size), packed.dtype),
            jax.ShapeDtypeStruct((width, width), packed.dtype),
            jax.ShapeDtypeStruct((width, FF), packed.dtype),
            jax.ShapeDtypeStruct((FF, width), packed.dtype),
            jax.ShapeDtypeStruct((total, VEC_ROWS, BLK), packed.dtype),
        ),
        in_specs=[pl.BlockSpec(memory_space=pltpu.SMEM), whole, whole],
        out_specs=(any_space, whole, whole, whole, whole, whole),
        scratch_shapes=[
            pltpu.VMEM((total * packed.shape[0],) + packed.shape[1:], packed.dtype),
            pltpu.SemaphoreType.DMA((2,)),
            pltpu.SemaphoreType.DMA((max(sends_x, 1),)),
            pltpu.SemaphoreType.DMA((head_size,)),
            pltpu.SemaphoreType.DMA((max(sends_w, 1),)),
            pltpu.SemaphoreType.DMA((total,)),
        ],
        compiler_params=pltpu.CompilerParams(
            collective_id=0, has_side_effects=True, vmem_limit_bytes=40 * 1024 * 1024
        ),
        name="gather_all",
    )(inverse, inputs, packed)


def scatter_kernel(
    dims,
    slots,
    owner_ref,
    blocks_ref,
    vec_ref,
    grad_ref,
    vec_out_ref,
    term,
    got_c,
    got_x,
    got_y,
    got_z,
    send_c,
    send_x,
    send_y,
    send_z,
    recv_c,
    recv_x,
    recv_y,
    recv_z,
):
    me = place(dims)
    size_z, size_x, size_y, size_c = dims
    rows = slots * BLK
    greet(dims, me)

    def block_of(dest, slot):
        owner = owner_ref[dest * slots + slot]
        block = blocks_ref[jnp.minimum(owner, NBLK - 1)]
        return jnp.where(owner < NBLK, block, jnp.zeros_like(block))

    def total_of(dest, extras, keep_block, keep_vec):
        def one(slot, carry):
            value = block_of(dest, slot).astype(jnp.float32)
            span = pl.ds(pl.multiple_of(slot * BLK, BLK), BLK)
            for ref, lead in extras:
                value = value + ref[lead + (span,)].astype(jnp.float32)
            keep_block(slot, span, value)
            return carry

        lax.fori_loop(0, slots, one, 0)
        value = vec_ref[dest].astype(jnp.float32)
        for ref, lead in extras:
            value = value + ref[lead + (pl.ds(rows, VEC_ROWS),)].astype(jnp.float32)
        keep_vec(value)

    def into_term(dest, extras):
        def keep_block(slot, span, value):
            term[dest, span] = value.astype(jnp.bfloat16)

        def keep_vec(value):
            term[dest, pl.ds(rows, VEC_ROWS)] = value.astype(jnp.bfloat16)

        total_of(dest, extras, keep_block, keep_vec)

    def remote(dest, got, send, recv, hop, index, target):
        return pltpu.make_async_remote_copy(
            src_ref=term.at[dest],
            dst_ref=got.at[hop, index],
            send_sem=send.at[hop, index],
            recv_sem=recv.at[hop, index],
            device_id=device(dims, target),
            device_id_type=MESH,
        )

    def each(axis, begin, end, coords_of, extras_of, got, send, recv, only=None):
        for step in range(1, dims[axis]) if only is None else [only]:
            target = moved(dims, me, axis, step)

            def one(index, carry, step=step, target=target):
                coords = list(coords_of(index))
                coords[axis] = target[axis]
                dest = flat(dims, coords)
                into_term(dest, extras_of(coords))
                remote(dest, got, send, recv, step - 1, index, target).start()
                return carry

            if end == begin + 1:
                one(begin, 0)
            else:
                lax.fori_loop(begin, end, one, 0)

    def wait_for(axis, got, send, recv, index):
        found = []
        for step in range(1, dims[axis]):
            remote(0, got, send, recv, step - 1, index, moved(dims, me, axis, step)).wait_recv()
            found.append((got, (step - 1, index)))
        return found

    def turn_z(order):
        return lax.rem(me[0] + 1 + order, size_z)

    def order_z(coords):
        return lax.rem(coords[0] - me[0] + 2 * size_z - 1, size_z)

    def index_c(coords):
        order_x = lax.rem(coords[1] - me[1] + size_x - 1 + size_x, size_x)
        return (order_z(coords) * size_x + order_x) * size_y + coords[2]

    def coords_c(index):
        order_x = lax.rem(lax.div(index, size_y), size_x)
        return (
            turn_z(lax.div(index, size_x * size_y)),
            lax.rem(me[1] + 1 + order_x, size_x),
            lax.rem(index, size_y),
            me[3],
        )

    def coords_x(index):
        return (turn_z(lax.div(index, size_y)), me[1], lax.rem(index, size_y), me[3])

    def coords_y(index):
        return (turn_z(index), me[1], me[2], me[3])

    def coords_z(index):
        return me

    def extras_c(coords):
        return []

    def extras_x(coords):
        return wait_for(3, got_c, send_c, recv_c, index_c(coords))

    def extras_y(coords):
        return extras_x(coords) + wait_for(
            1, got_x, send_x, recv_x, order_z(coords) * size_y + coords[2]
        )

    def extras_z(coords):
        return extras_y(coords) + wait_for(2, got_y, send_y, recv_y, order_z(coords))

    def stage_c(order):
        group = size_x * size_y
        each(3, order * group, (order + 1) * group, coords_c, extras_c, got_c, send_c, recv_c)

    def stage_x(order):
        group = size_y
        each(1, order * group, (order + 1) * group, coords_x, extras_x, got_x, send_x, recv_x)

    stage_c(0)
    for order in range(1, size_z):
        stage_c(order)
        stage_x(order - 1)
    stage_x(size_z - 1)
    for order in range(size_z):
        each(2, order, order + 1, coords_y, extras_y, got_y, send_y, recv_y)
        if order + 1 < size_z:
            each(0, 0, 1, coords_z, extras_z, got_z, send_z, recv_z, only=order + 1)
    extras = extras_z(me) + wait_for(0, got_z, send_z, recv_z, 0)

    def keep_block(slot, span, value):
        grad_ref[slot] = value

    def keep_vec(value):
        vec_out_ref[...] = value

    total_of(flat(dims, me), extras, keep_block, keep_vec)

    def drain(axis, count, got, send, recv):
        for step in range(1, dims[axis]):

            def one(index, carry, step=step):
                remote(
                    0, got, send, recv, step - 1, index, moved(dims, me, axis, step)
                ).wait_send()
                return carry

            lax.fori_loop(0, count, one, 0)

    drain(3, size_z * size_x * size_y, got_c, send_c, recv_c)
    drain(1, size_z * size_y, got_x, send_x, recv_x)
    drain(2, size_z, got_y, send_y, recv_y)
    drain(0, 1, got_z, send_z, recv_z)


def scatter_sums(dims, owner_slot, blocks, vec_terms):
    size_z, size_x, size_y, size_c = dims
    total = size_z * size_x * size_y * size_c
    slots = owner_slot.shape[0] // total
    chunk = (slots * BLK + VEC_ROWS, BLK)
    shapes = [
        (max(size_c - 1, 1), size_z * size_x * size_y),
        (max(size_x - 1, 1), size_z * size_y),
        (max(size_y - 1, 1), size_z),
        (max(size_z - 1, 1), 1),
    ]
    whole = pl.BlockSpec(memory_space=pltpu.VMEM)
    return pl.pallas_call(
        functools.partial(scatter_kernel, dims, slots),
        out_shape=(
            jax.ShapeDtypeStruct((slots, BLK, BLK), jnp.float32),
            jax.ShapeDtypeStruct((VEC_ROWS, BLK), jnp.float32),
        ),
        in_specs=[pl.BlockSpec(memory_space=pltpu.SMEM), whole, whole],
        out_specs=(whole, whole),
        scratch_shapes=[pltpu.VMEM((total,) + chunk, jnp.bfloat16)]
        + [pltpu.VMEM(shape + chunk, jnp.bfloat16) for shape in shapes]
        + [pltpu.SemaphoreType.DMA(shape) for shape in shapes]
        + [pltpu.SemaphoreType.DMA(shape) for shape in shapes],
        compiler_params=pltpu.CompilerParams(
            collective_id=1, has_side_effects=True, vmem_limit_bytes=60 * 1024 * 1024
        ),
        name="scatter_sums",
    )(owner_slot, blocks, vec_terms)


def three_parts(values):
    high = lax.reduce_precision(values, 8, 7)
    rest = values - high
    middle = lax.reduce_precision(rest, 8, 7)
    low = lax.reduce_precision(rest - middle, 8, 7)
    return [part.astype(jnp.bfloat16) for part in (high, middle, low)]


def as_rows(vector, rows):
    return jnp.pad(vector, (0, rows * BLK - vector.shape[0])).reshape(rows, BLK)


def ceil_to(value, unit):
    return -(-value // unit) * unit


def body(
    inputs,
    cotangent,
    span_offset,
    span_len,
    owner_slot,
    master,
    moment_one,
    moment_two,
    basis_left,
    basis_right,
    average,
    vec_master,
    vec_moment_one,
    vec_moment_two,
):
    both = ("seq", "head")
    seq_size = lax.axis_size("seq")
    head_size = lax.axis_size("head")
    total = seq_size * head_size
    head_index = lax.axis_index("head")
    seq_local, tok_local, width = inputs.shape
    slots_local = master.shape[0]
    slot_total = slots_local * total
    vec_local = vec_master.shape[0]

    dims = cut(seq_size, head_size)

    packed = jnp.concatenate(
        [
            master.astype(jnp.bfloat16).reshape(slots_local * BLK, BLK),
            as_rows(jnp.concatenate(three_parts(vec_master)), VEC_ROWS),
        ],
        0,
    ).reshape(-1, PIECE, BLK)
    numbers = jnp.arange(slot_total, dtype=jnp.int32)
    inverse = jnp.sum(
        jnp.where(owner_slot[:, None] == numbers[None, :], numbers[:, None], 0), axis=0
    )
    pieces = (inverse // slots_local) * packed.shape[0]
    pieces = pieces + (inverse % slots_local) * (BLK // PIECE)
    inputs_full, w_qkv, w_out, w_up, w_down, vec_parts = gather_all(
        dims, pieces, inputs, packed
    )
    parts = (
        vec_parts
        .reshape(total, VEC_ROWS * BLK)[:, : 3 * vec_local]
        .reshape(total, 3, vec_local)
        .astype(jnp.float32)
    )
    all_vector = ((parts[:, 2] + parts[:, 1]) + parts[:, 0]).reshape(-1)

    b_query, b_value, b_out, gain_one, shift_one, b_up, b_down, gain_two, shift_two = split_vector(
        all_vector
    )
    token_rows = inputs.reshape(seq_local * tok_local, width)
    local_shape = (seq_local, tok_local, width)
    cols = width // head_size
    begin = head_index * cols

    def own(array):
        return lax.dynamic_slice_in_dim(array, begin, cols, array.ndim - 1)

    w_own = lax.dynamic_index_in_dim(w_qkv, head_index, 0, keepdims=False)
    b_own = jnp.concatenate([own(b_query), jnp.zeros((cols,), jnp.float32), own(b_value)], 0)
    qkv, context, log_total = attend(inputs_full, w_own, b_own[None, :])
    context_rows = context.transpose(1, 2, 0, 3).reshape(seq_local * tok_local, width)
    branch = jnp.dot(context_rows, w_out, preferred_element_type=jnp.float32) + b_out
    z_one = token_rows.astype(jnp.float32) + branch
    first = layer_norm(z_one, gain_one, shift_one)
    first_low = first.astype(jnp.bfloat16)
    hidden_in = jnp.dot(first_low, w_up, preferred_element_type=jnp.float32) + b_up
    hidden_act = gelu_value(hidden_in).astype(jnp.bfloat16)
    ffn_out = jnp.dot(hidden_act, w_down, preferred_element_type=jnp.float32) + b_down
    z_two = first + ffn_out
    result, pull_two = jax.vjp(layer_norm, z_two, gain_two, shift_two)
    layer_out = result.astype(jnp.bfloat16).reshape(local_shape)
    mask = span_mask(span_offset, span_len)
    grad_out = (cotangent.astype(jnp.float32) * mask[:, :, None]).reshape(
        seq_local * tok_local, width
    )
    d_ztwo, d_gain_two, d_shift_two = pull_two(grad_out)
    d_ffn = d_ztwo.astype(jnp.bfloat16)
    grad_bdown = jnp.sum(d_ffn.astype(jnp.float32), axis=0)
    d_hidden = back_product(d_ffn, w_down)
    d_hidden_in = (d_hidden * gelu_slope(hidden_in)).astype(jnp.bfloat16)
    grad_bup = jnp.sum(d_hidden_in.astype(jnp.float32), axis=0)
    d_first = d_ztwo + back_product(d_hidden_in, w_up)
    sink, pull_one = jax.vjp(layer_norm, z_one, gain_one, shift_one)
    d_zone, d_gain_one, d_shift_one = pull_one(d_first)
    d_branch = d_zone.astype(jnp.bfloat16)
    grad_bout = jnp.sum(d_branch.astype(jnp.float32), axis=0)

    blocks, grad_b_own, input_grad = backward(
        d_branch,
        w_out,
        w_qkv,
        log_total,
        d_zone,
        d_ffn,
        first_low,
        context,
        hidden_act,
        d_hidden_in,
        inputs_full,
        qkv,
    )
    grad_b_own = grad_b_own.reshape(-1)

    def put(array):
        empty = jnp.zeros(array.shape[:-1] + (width,), array.dtype)
        return lax.dynamic_update_slice_in_dim(empty, array, begin, array.ndim - 1)

    vector_terms = jnp.concatenate(
        [
            put(grad_b_own[:cols]),
            put(grad_b_own[2 * cols :]),
            grad_bout,
            d_gain_one,
            d_shift_one,
            grad_bup,
            grad_bdown,
            d_gain_two,
            d_shift_two,
        ],
        0,
    ).reshape(total, vec_local)
    vec_terms = jnp.pad(vector_terms, ((0, 0), (0, VEC_ROWS * BLK - vec_local)))
    vec_terms = vec_terms.astype(jnp.bfloat16).reshape(total, VEC_ROWS, BLK)
    slot_grad, vec_sums = scatter_sums(dims, owner_slot, blocks, vec_terms)
    vec_grad = vec_sums.reshape(-1)[:vec_local]
    first_moment, second_moment, updated = rotate_adam(
        slot_grad, master, moment_one, moment_two, basis_left, basis_right
    )
    correct = 1.0 - 0.5**STEP
    vec_first = 0.5 * vec_moment_one + 0.5 * vec_grad
    vec_second = 0.5 * vec_moment_two + 0.5 * vec_grad * vec_grad
    vec_new = vec_master - VEC_RATE * (vec_first / correct) / (
        jnp.sqrt(vec_second / correct) + ADAM_EPS
    )
    new_average = KEEP * average + (1.0 - KEEP) * updated
    return (
        layer_out,
        input_grad,
        slot_grad,
        vec_grad,
        first_moment,
        second_moment,
        updated,
        updated.astype(jnp.bfloat16),
        new_average,
        vec_first,
        vec_second,
        vec_new,
    )


def solution(mesh):
    placed = (
        P("seq", "head", None),
        P("seq", "head", None),
        P("seq", "head"),
        P("seq", "head"),
        P(),
        P(("seq", "head"), None, None),
        P(("seq", "head"), None, None),
        P(("seq", "head"), None, None),
        P(("seq", "head"), None, None),
        P(("seq", "head"), None, None),
        P(("seq", "head"), None, None),
        P(("seq", "head")),
        P(("seq", "head")),
        P(("seq", "head")),
    )
    return jax.shard_map(
        body,
        mesh=mesh,
        in_specs=placed,
        out_specs=(
            P("seq", "head", None),
            P("seq", "head", None),
            P(("seq", "head"), None, None),
            P(("seq", "head")),
            P(("seq", "head"), None, None),
            P(("seq", "head"), None, None),
            P(("seq", "head"), None, None),
            P(("seq", "head"), None, None),
            P(("seq", "head"), None, None),
            P(("seq", "head")),
            P(("seq", "head")),
            P(("seq", "head")),
        ),
        check_vma=False,
    )
```

profile of v0, /device:TPU:11, one launch (start us, length us, event | category | flops | bytes accessed | tf_op | source)
XLA Modules:
  0.0 263.9 jit_solution(215861098948986067)
XLA Ops:
  0.7 0.8 broadcast_in_dim.32
  1.6 0.8 broadcast_in_dim.33
  2.5 2.6 fusion.19
  5.4 71.6 %gather_all.1 = (bf16[3,4,256,512]{3,2,1,0:T(8,128)(2,1)S(1)}, bf16[4,512,384]{2,1,0:T(8,128)(2,1)S(1)}, bf16[512,512]{1,0:T(8,128)(2,1)S(1)}, bf16[512,2048]{1,...) custom-call(s32[256]{0:T(256)S(1)} %fusion.37.inv_ref, ...), custom_call_target="tpu_custom_call" | custom-call | tf_op jit(solution)/shard_map/gather_all/pallas_call | solution.py:683
  77.0 1.7 copy-done.1
  78.6 0.8 copy-done.7
  79.4 1.3 copy-done.10
  80.8 1.3 copy-done.12
  82.7 29.0 %attend.1 = (bf16[3,1024,384]{2,1,0:T(8,128)(2,1)S(1)}, bf16[4,3,256,128]{3,2,1,0:T(8,128)(2,1)S(1)}, f32[3,8,1024]{2,1,0:T(8,128)S(1)}) custom-call(bf16[3,4,256,512]{3,2,1,0:T(8,128)(2,1)} %copy-done.1, bf16[512,384]{1,0:T(8,128)(2,1)S(1)} %dynamic-slice_bitcast_fusion.w_ref, f32[1,384]{1,0:T(1,128)S(1)} %broadcast_in_dim.31.b_ref), custom_call_target="tpu_custom_call" | custom-call | tf_op jit(solution)/shard_map/attend/pallas_call | solution.py:151
  112.4 1.1 copy-done.6
  114.0 0.7 fusion.46
  115.4 1.5 copy-done.11
  116.9 3.3 %multiply_convert_fusion = (bf16[768,2048]{1,0:T(8,128)(2,1)S(1)}, f32[768,2048]{1,0:T(8,128)S(1)}) fusion(f32[2048]{0:T(1024)S(1)} %slice.81, bf16[768,512]{1,0:T(8,128)(2,1)S(1)} %fusion.7.yb_ref, bf16[512,2048]{1,0:T(8,128)(2,1)S(1)} %copy-done.11), kind=kOutput, calls=%fused_computation.7 | convolution fusion | flops 1620049920 | bytes 12328960 | tf_op jit(solution)/shard_map/dot_general | solution.py:1004
  120.3 1.6 copy-done.17
  121.9 2.1 fusion.47
  124.4 1.0 copy-done.14
  126.0 1.6 fusion.44
  127.8 4.4 %fusion.48 = (bf16[2048]{0:T(1024)(128)(2,1)S(1)}, bf16[768,2048]{1,0:T(8,128)(2,1)S(1)}) fusion(f32[768,2048]{1,0:T(8,128)S(1)} %get-tuple-element.79, f32[2048]{0:T(1024)S(1)} %slice.81, bf16[768,512]{1,0:T(8,128)(2,1)S(1)} %get-tuple-element.50.df_ref, bf16[2048,512]{1,0:T(8,128)(2,1)S(1)} %copy-done.13), kind=kOutput, calls=%fused_computation.106 | convolution fusion | flops 1629485056 | bytes 12333056 | tf_op jit(solution)/shard_map/to,io->ti/dot_general | solution.py:424
  132.2 2.4 multiply_reduce_fusion
  135.3 1.7 fusion.42
  137.0 51.8 %backward.1 = (bf16[192,128,128]{2,1,0:T(8,128)(2,1)}, f32[1,384]{1,0:T(1,128)}, f32[3,256,512]{2,1,0:T(8,128)}) custom-call(bf16[768,512]{1,0:T(8,128)(2,1)} %get-tuple-element.52.da_ref, bf16[512,512]{1,0:T(8,128)(2,1)} %copy-done.7, bf16[4,512,384]{2,1,0:T(8,128)(2,1)} %copy-done.3, f32[3,8,1024]{2,1,0:T(8,128)} %copy-done.9, ...), custom_call_target="tpu_custom_call" | custom-call | tf_op jit(solution)/shard_map/backward/pallas_call | solution.py:365
  188.8 0.7 bitcast_dynamic-update-slice_fusion.1
  189.8 0.7 bitcast_dynamic-update-slice_fusion
  192.5 0.7 copy.38
  193.2 60.3 %scatter_sums.1 = (f32[8,128,128]{2,1,0:T(8,128)}, f32[16,128]{1,0:T(8,128)}) custom-call(s32[256]{0:T(256)} %owner_ref.1, bf16[192,128,128]{2,1,0:T(8,128)(2,1)} %get-tuple-element.36.blocks_ref, bf16[32,16,128]{2,1,0:T(8,128)(2,1)} %bitcast.62), custom_call_target="tpu_custom_call" | custom-call | tf_op jit(solution)/shard_map/scatter_sums/pallas_call | solution.py:898
  253.6 1.4 divide_subtract_fusion
  254.9 2.0 fusion.49
  257.0 0.7 fusion.12
  257.8 0.9 fusion.13
  259.4 2.3 multiply_add_fusion.2
  261.7 1.1 copy.60
  263.1 0.8 copy.61
  (112 shorter events, 8.0 us)
Async XLA Ops:
  0.6 256.3 %copy-start = (f32[8,128,128]{2,1,0:T(8,128)S(1)}, f32[8,128,128]{2,1,0:T(8,128)}, u32[]{:S(2)}) copy-start(f32[8,128,128]{2,1,0:T(8,128)} %param.23) | copy-start | bytes 1572868
  0.7 4.4 %copy-start.30 = (s32[256]{0:T(256)S(1)}, s32[256]{0:T(256)}, u32[]{:S(2)}) copy-start(s32[256]{0:T(256)} %owner_ref.1) | copy-start | bytes 3076
  0.7 4.5 %copy-start.29 = (f32[192]{0:T(256)S(1)}, f32[192]{0:T(256)}, u32[]{:S(2)}) copy-start(f32[192]{0:T(256)} %param.25) | copy-start | bytes 2308
  0.7 4.6 %copy-start.20 = (f32[8,128,128]{2,1,0:T(8,128)S(1)}, f32[8,128,128]{2,1,0:T(8,128)}, u32[]{:S(2)}) copy-start(f32[8,128,128]{2,1,0:T(8,128)} %param.19) | copy-start | bytes 1572868
  2.5 2.9 %copy-start.5 = (bf16[3,256,512]{2,1,0:T(8,128)(2,1)S(1)}, bf16[3,256,512]{2,1,0:T(8,128)(2,1)}, u32[]{:S(2)}) copy-start(bf16[3,256,512]{2,1,0:T(8,128)(2,1)} %x_ref.1) | copy-start | bytes 2359300
  76.9 1.7 copy-start.1
  79.4 1.3 copy-start.10
  80.8 1.3 copy-start.12
  82.1 29.6 %copy-start.3 = (bf16[4,512,384]{2,1,0:T(8,128)(2,1)}, bf16[4,512,384]{2,1,0:T(8,128)(2,1)S(1)}, u32[]{:S(2)}) copy-start(bf16[4,512,384]{2,1,0:T(8,128)(2,1)S(1)} %get-tuple-element.27.w_ref) | copy-start | bytes 4718596
  111.7 3.0 %copy-start.2 = (bf16[4,3,256,128]{3,2,1,0:T(8,128)(2,1)}, bf16[4,3,256,128]{3,2,1,0:T(8,128)(2,1)S(1)}, u32[]{:S(2)}) copy-start(bf16[4,3,256,128]{3,2,1,0:T(8,128)(2,1)S(1)} %get-tuple-element.29.ctx_ref) | copy-start | bytes 2359300
  111.7 3.0 %copy-start.4 = (bf16[3,1024,384]{2,1,0:T(8,128)(2,1)}, bf16[3,1024,384]{2,1,0:T(8,128)(2,1)S(1)}, u32[]{:S(2)}) copy-start(bf16[3,1024,384]{2,1,0:T(8,128)(2,1)S(1)} %get-tuple-element.34.qkv_any) | copy-start | bytes 7077892
  111.7 3.0 %copy-start.9 = (f32[3,8,1024]{2,1,0:T(8,128)}, f32[3,8,1024]{2,1,0:T(8,128)S(1)}, u32[]{:S(2)}) copy-start(f32[3,8,1024]{2,1,0:T(8,128)S(1)} %get-tuple-element.33.lse_ref) | copy-start | bytes 294916
  111.7 1.7 copy-start.6
  111.8 2.2 copy-start.8
  115.1 1.9 copy-start.11
  115.4 4.9 %copy-start.15 = (bf16[768,512]{1,0:T(8,128)(2,1)}, bf16[768,512]{1,0:T(8,128)(2,1)S(1)}, u32[]{:S(2)}) copy-start(bf16[768,512]{1,0:T(8,128)(2,1)S(1)} %fusion.7.yb_ref) | copy-start | bytes 2359300
  116.9 5.0 %copy-start.13 = (bf16[2048,512]{1,0:T(8,128)(2,1)S(1)}, bf16[2048,512]{1,0:T(8,128)(2,1)}, u32[]{:S(2)}) copy-start(bf16[2048,512]{1,0:T(8,128)(2,1)} %copy-done.12) | copy-start | bytes 6291460
  120.3 1.6 copy-start.17
  124.0 1.4 copy-start.14
  127.8 4.4 %copy-start.16 = (bf16[768,512]{1,0:T(8,128)(2,1)}, bf16[768,512]{1,0:T(8,128)(2,1)S(1)}, u32[]{:S(2)}) copy-start(bf16[768,512]{1,0:T(8,128)(2,1)S(1)} %get-tuple-element.50.df_ref) | copy-start | bytes 2359300
  132.2 2.5 copy-start.18
  193.2 60.3 %copy-start.31 = (f32[192]{0:T(256)S(1)}, f32[192]{0:T(256)}, u32[]{:S(2)}) copy-start(f32[192]{0:T(256)} %param.27) | copy-start | bytes 2308
  193.2 60.3 %copy-start.32 = (f32[192]{0:T(256)S(1)}, f32[192]{0:T(256)}, u32[]{:S(2)}) copy-start(f32[192]{0:T(256)} %param.26) | copy-start | bytes 2308
  193.2 61.7 %copy-start.23 = (f32[8,128,128]{2,1,0:T(8,128)S(1)}, f32[8,128,128]{2,1,0:T(8,128)}, u32[]{:S(2)}) copy-start(f32[8,128,128]{2,1,0:T(8,128)} %param.22) | copy-start | bytes 1572868
  253.5 3.5 %copy-start.24 = (f32[8,128,128]{2,1,0:T(8,128)S(1)}, f32[8,128,128]{2,1,0:T(8,128)}, u32[]{:S(2)}) copy-start(f32[8,128,128]{2,1,0:T(8,128)} %param.21) | copy-start | bytes 1572868
  253.5 3.5 %copy-start.25 = (f32[8,128,128]{2,1,0:T(8,128)S(1)}, f32[8,128,128]{2,1,0:T(8,128)}, u32[]{:S(2)}) copy-start(f32[8,128,128]{2,1,0:T(8,128)} %param.20) | copy-start | bytes 1572868
  257.7 3.9 %copy-start.27 = (f32[8,128,128]{2,1,0:T(8,128)}, f32[8,128,128]{2,1,0:T(8,128)S(1)}, u32[]{:S(2)}) copy-start(f32[8,128,128]{2,1,0:T(8,128)S(1)} %get-tuple-element.103) | copy-start | bytes 1572868
  257.8 3.9 %copy-start.28 = (f32[8,128,128]{2,1,0:T(8,128)}, f32[8,128,128]{2,1,0:T(8,128)S(1)}, u32[]{:S(2)}) copy-start(f32[8,128,128]{2,1,0:T(8,128)S(1)} %get-tuple-element.102) | copy-start | bytes 1572868
  257.8 1.4 copy-start.21
  257.8 1.6 copy-start.26
  259.4 2.4 copy-start.22
  261.7 1.4 copy-start.19
  (1 other events, 0.8 us)
where the time goes:
time: 267 us; the launch traced here: 264 us
  Pallas kernels  213 us (80%)
  local copies, waits for them, and re-layouts  21.1 us (8%)
  matrix products  18.9 us (7%)
  other arithmetic  10.1 us (4%)
    pallas_call x1, Pallas kernels, gather_all(): pl.pallas_call(functools.partial(gather_kernel, dims), out_shape=(jax.Sha...  71.6 us
    pallas_call x1, Pallas kernels, scatter_sums(): pl.pallas_call(functools.partial(scatter_kernel, dims, slots), out_shape=...  60.3 us
    pallas_call x1, Pallas kernels, backward(): pl.pallas_call(backward_kernel, out_shape=(jax.ShapeDtypeStruct((NBLK, BL...  51.8 us
    pallas_call x1, Pallas kernels, attend(): pl.pallas_call(forward_kernel, grid=(seq_local,), out_shape=(jax.ShapeDty...  29 us
    unnamed x79, local copies, waits for them, and re-layouts  16.6 us
    dot_general x2, matrix products, back_product(): jnp.einsum('to,io->ti', grads, weight, preferred_element_type=jnp.float32)  6.8 us

commit v1 on v0

--- a/solution.py
+++ b/solution.py
@@ -407,17 +407,63 @@
     )
 
 
-def rotate_adam(grads, master, moment_one, moment_two, basis_left, basis_right):
-    rotated = jnp.einsum("sji,sjk->sik", basis_left, grads, precision=HIGH)
-    rotated = jnp.einsum("sik,skl->sil", rotated, basis_right, precision=HIGH)
-    first = 0.5 * moment_one + 0.5 * rotated
-    second = 0.5 * moment_two + 0.5 * rotated * rotated
+def high_product(left, right, left_axis, right_axis):
+    return lax.dot_general(
+        left,
+        right,
+        (((left_axis,), (right_axis,)), ((), ())),
+        precision=HIGH,
+        preferred_element_type=jnp.float32,
+    )
+
+
+def adam_kernel(
+    grad_ref,
+    master_ref,
+    one_ref,
+    two_ref,
+    left_ref,
+    right_ref,
+    average_ref,
+    new_one_ref,
+    new_two_ref,
+    new_master_ref,
+    new_short_ref,
+    new_average_ref,
+):
+    slots = range(grad_ref.shape[0])
     correct = 1.0 - 0.5**STEP
-    normed = first / correct / (jnp.sqrt(second / correct) + ADAM_EPS)
-    turned = jnp.einsum("sij,sjk->sik", basis_left, normed, precision=HIGH)
-    turned = jnp.einsum("sik,slk->sil", turned, basis_right, precision=HIGH)
-    updated = master - RATE * (turned + DECAY * master)
-    return (first, second, updated)
+    rotated = [high_product(left_ref[slot], grad_ref[slot], 0, 0) for slot in slots]
+    rotated = [high_product(rotated[slot], right_ref[slot], 1, 0) for slot in slots]
+    normed = []
+    for slot in slots:
+        first = 0.5 * one_ref[slot] + 0.5 * rotated[slot]
+        second = 0.5 * two_ref[slot] + 0.5 * rotated[slot] * rotated[slot]
+        new_one_ref[slot] = first
+        new_two_ref[slot] = second
+        normed.append(first / correct / (jnp.sqrt(second / correct) + ADAM_EPS))
+    turned = [high_product(left_ref[slot], normed[slot], 1, 0) for slot in slots]
+    turned = [high_product(turned[slot], right_ref[slot], 1, 1) for slot in slots]
+    for slot in slots:
+        updated = master_ref[slot] - RATE * (turned[slot] + DECAY * master_ref[slot])
+        new_master_ref[slot] = updated
+        new_short_ref[slot] = updated.astype(jnp.bfloat16)
+        new_average_ref[slot] = KEEP * average_ref[slot] + (1.0 - KEEP) * updated
+
+
+def adam(grads, master, moment_one, moment_two, basis_left, basis_right, average):
+    slots = grads.shape[0]
+    together = math.gcd(slots, 4)
+    spec = pl.BlockSpec((together, BLK, BLK), lambda s: (s, 0, 0))
+    full = jax.ShapeDtypeStruct(grads.shape, jnp.float32)
+    return pl.pallas_call(
+        adam_kernel,
+        grid=(slots // together,),
+        out_shape=(full, full, full, jax.ShapeDtypeStruct(grads.shape, jnp.bfloat16), full),
+        in_specs=[spec] * 7,
+        out_specs=(spec,) * 5,
+        name="adam",
+    )(grads, master, moment_one, moment_two, basis_left, basis_right, average)
 
 
 def back_product(grads, weight):
@@ -797,74 +843,87 @@
             found.append((got, (step - 1, index)))
         return found
 
-    def turn_z(order):
-        return lax.rem(me[0] + 1 + order, size_z)
-
-    def order_z(coords):
-        return lax.rem(coords[0] - me[0] + 2 * size_z - 1, size_z)
+    def turned(axis, order):
+        return lax.rem(me[axis] + 1 + order, dims[axis])
+
+    def order_of(axis, coords):
+        return lax.rem(coords[axis] - me[axis] + 2 * dims[axis] - 1, dims[axis])
 
     def index_c(coords):
-        order_x = lax.rem(coords[1] - me[1] + size_x - 1 + size_x, size_x)
-        return (order_z(coords) * size_x + order_x) * size_y + coords[2]
+        return (order_of(0, coords) * size_x + order_of(1, coords)) * size_y + order_of(2, coords)
 
     def coords_c(index):
-        order_x = lax.rem(lax.div(index, size_y), size_x)
         return (
-            turn_z(lax.div(index, size_x * size_y)),
-            lax.rem(me[1] + 1 + order_x, size_x),
-            lax.rem(index, size_y),
+            turned(0, lax.div(index, size_x * size_y)),
+            turned(1, lax.rem(lax.div(index, size_y), size_x)),
+            turned(2, lax.rem(index, size_y)),
             me[3],
         )
 
-    def coords_x(index):
-        return (turn_z(lax.div(index, size_y)), me[1], lax.rem(index, size_y), me[3])
-
-    def coords_y(index):
-        return (turn_z(index), me[1], me[2], me[3])
-
-    def coords_z(index):
-        return me
-
-    def extras_c(coords):
-        return []
-
-    def extras_x(coords):
-        return wait_for(3, got_c, send_c, recv_c, index_c(coords))
-
-    def extras_y(coords):
-        return extras_x(coords) + wait_for(
-            1, got_x, send_x, recv_x, order_z(coords) * size_y + coords[2]
-        )
-
-    def extras_z(coords):
-        return extras_y(coords) + wait_for(2, got_y, send_y, recv_y, order_z(coords))
-
-    def stage_c(order):
-        group = size_x * size_y
-        each(3, order * group, (order + 1) * group, coords_c, extras_c, got_c, send_c, recv_c)
-
-    def stage_x(order):
-        group = size_y
-        each(1, order * group, (order + 1) * group, coords_x, extras_x, got_x, send_x, recv_x)
-
-    stage_c(0)
-    for order in range(1, size_z):
-        stage_c(order)
-        stage_x(order - 1)
-    stage_x(size_z - 1)
-    for order in range(size_z):
-        each(2, order, order + 1, coords_y, extras_y, got_y, send_y, recv_y)
-        if order + 1 < size_z:
-            each(0, 0, 1, coords_z, extras_z, got_z, send_z, recv_z, only=order + 1)
-    extras = extras_z(me) + wait_for(0, got_z, send_z, recv_z, 0)
-
-    def keep_block(slot, span, value):
-        grad_ref[slot] = value
-
-    def keep_vec(value):
-        vec_out_ref[...] = value
-
-    total_of(flat(dims, me), extras, keep_block, keep_vec)
+    def run(first, second):
+        size_s = dims[second]
+
+        def coords_f(index):
+            coords = list(me)
+            coords[0] = turned(0, lax.div(index, size_s))
+            coords[second] = turned(second, lax.rem(index, size_s))
+            return coords
+
+        def coords_s(index):
+            coords = list(me)
+            coords[0] = turned(0, index)
+            return coords
+
+        def coords_z(index):
+            return me
+
+        def extras_c(coords):
+            return []
+
+        def extras_f(coords):
+            return wait_for(3, got_c, send_c, recv_c, index_c(coords))
+
+        def extras_s(coords):
+            index = order_of(0, coords) * size_s + order_of(second, coords)
+            return extras_f(coords) + wait_for(first, got_x, send_x, recv_x, index)
+
+        def extras_z(coords):
+            return extras_s(coords) + wait_for(
+                second, got_y, send_y, recv_y, order_of(0, coords)
+            )
+
+        def stage_c(order):
+            group = size_x * size_y
+            each(3, order * group, (order + 1) * group, coords_c, extras_c, got_c, send_c, recv_c)
+
+        def stage_f(order):
+            group = size_s
+            each(
+                first, order * group, (order + 1) * group, coords_f, extras_f, got_x, send_x, recv_x
+            )
+
+        stage_c(0)
+        for order in range(1, size_z):
+            stage_c(order)
+            stage_f(order - 1)
+        stage_f(size_z - 1)
+        for order in range(size_z):
+            each(second, order, order + 1, coords_s, extras_s, got_y, send_y, recv_y)
+            if order + 1 < size_z:
+                each(0, 0, 1, coords_z, extras_z, got_z, send_z, recv_z, only=order + 1)
+        extras = extras_z(me) + wait_for(0, got_z, send_z, recv_z, 0)
+
+        def keep_block(slot, span, value):
+            grad_ref[slot] = value
+
+        def keep_vec(value):
+            vec_out_ref[...] = value
+
+        total_of(flat(dims, me), extras, keep_block, keep_vec)
+        drain(3, size_z * size_x * size_y, got_c, send_c, recv_c)
+        drain(first, size_z * size_s, got_x, send_x, recv_x)
+        drain(second, size_z, got_y, send_y, recv_y)
+        drain(0, 1, got_z, send_z, recv_z)
 
     def drain(axis, count, got, send, recv):
         for step in range(1, dims[axis]):
@@ -877,10 +936,11 @@
 
             lax.fori_loop(0, count, one, 0)
 
-    drain(3, size_z * size_x * size_y, got_c, send_c, recv_c)
-    drain(1, size_z * size_y, got_x, send_x, recv_x)
-    drain(2, size_z, got_y, send_y, recv_y)
-    drain(0, 1, got_z, send_z, recv_z)
+    for core in range(size_c):
+
+        @pl.when(me[3] == core)
+        def _(core=core):
+            run(1 + core % 2, 2 - core % 2)
 
 
 def scatter_sums(dims, owner_slot, blocks, vec_terms):
@@ -890,8 +950,8 @@
     chunk = (slots * BLK + VEC_ROWS, BLK)
     shapes = [
         (max(size_c - 1, 1), size_z * size_x * size_y),
-        (max(size_x - 1, 1), size_z * size_y),
-        (max(size_y - 1, 1), size_z),
+        (max(size_x - 1, size_y - 1, 1), size_z * max(size_x, size_y)),
+        (max(size_x - 1, size_y - 1, 1), size_z),
         (max(size_z - 1, 1), 1),
     ]
     whole = pl.BlockSpec(memory_space=pltpu.VMEM)
@@ -1061,8 +1121,8 @@
     vec_terms = vec_terms.astype(jnp.bfloat16).reshape(total, VEC_ROWS, BLK)
     slot_grad, vec_sums = scatter_sums(dims, owner_slot, blocks, vec_terms)
     vec_grad = vec_sums.reshape(-1)[:vec_local]
-    first_moment, second_moment, updated = rotate_adam(
-        slot_grad, master, moment_one, moment_two, basis_left, basis_right
+    first_moment, second_moment, updated, updated_short, new_average = adam(
+        slot_grad, master, moment_one, moment_two, basis_left, basis_right, average
     )
     correct = 1.0 - 0.5**STEP
     vec_first = 0.5 * vec_moment_one + 0.5 * vec_grad
@@ -1070,7 +1130,6 @@
     vec_new = vec_master - VEC_RATE * (vec_first / correct) / (
         jnp.sqrt(vec_second / correct) + ADAM_EPS
     )
-    new_average = KEEP * average + (1.0 - KEEP) * updated
     return (
         layer_out,
         input_grad,
@@ -1079,7 +1138,7 @@
         first_moment,
         second_moment,
         updated,
-        updated.astype(jnp.bfloat16),
+        updated_short,
         new_average,
         vec_first,
         vec_second,

time: 267 us -> 252 us (0.944)
  Pallas kernels: 213 us -> 205 us
  matrix products: 18.9 us -> 12.7 us
  local copies, waits for them, and re-layouts: 21.1 us -> 18.1 us
    pallas_call x1, Pallas kernels: 60.3 us -> 47.4 us  [scatter_sums(): pl.pallas_call(functools.partial(scatter_kernel, dims, slots), out_shape=...]
    dot_general x4 -> x0, matrix products: 6.02 us -> none  [the longest x1 2.34 us: rotate_adam(): turned = jnp.einsum('sik,slk->sil', turned, basis_right, precision=HIGH)]
    pallas_call x0 -> x1, Pallas kernels: none -> 5.67 us  [adam(): pl.pallas_call(adam_kernel, grid=(slots // together,), out_shape=(full, f...]
    unnamed x79 -> x59, local copies, waits for them, and re-layouts: 16.6 us -> 13.6 us
where the time goes in v1:
time: 252 us; the launch traced here: 247 us
  Pallas kernels  205 us (81%)
  local copies, waits for them, and re-layouts  18.1 us (7%)
  matrix products  12.7 us (5%)
  other arithmetic  9.95 us (4%)
    pallas_call x1, Pallas kernels, gather_all(): pl.pallas_call(functools.partial(gather_kernel, dims), out_shape=(jax.Sha...  71.6 us
    pallas_call x1, Pallas kernels, backward(): pl.pallas_call(backward_kernel, out_shape=(jax.ShapeDtypeStruct((NBLK, BL...  51.8 us
    pallas_call x1, Pallas kernels, scatter_sums(): pl.pallas_call(functools.partial(scatter_kernel, dims, slots), out_shape=...  47.4 us
    pallas_call x1, Pallas kernels, attend(): pl.pallas_call(forward_kernel, grid=(seq_local,), out_shape=(jax.ShapeDty...  29 us
    unnamed x59, local copies, waits for them, and re-layouts  13.6 us
    dot_general x2, matrix products, back_product(): jnp.einsum('to,io->ti', grads, weight, preferred_element_type=jnp.float32)  6.68 us
    pallas_call x1, Pallas kernels, adam(): pl.pallas_call(adam_kernel, grid=(slots // together,), out_shape=(full, f...  5.67 us

profile of v1, /device:TPU:11, one launch (start us, length us, event | category | flops | bytes accessed | tf_op | source)
XLA Modules:
  0.0 247.3 jit_solution(15024920884160508288)
XLA Ops:
  0.7 0.8 broadcast_in_dim.32
  1.6 0.8 broadcast_in_dim.33
  2.4 2.6 %fusion.10 = (bf16[512]{0:T(512)(128)(2,1)S(1)}, f32[3,256,512]{2,1,0:T(8,128)}) fusion(f32[3,256]{1,0:T(4,128)S(1)} %fusion.19, bf16[3,256,512]{2,1,0:T(8,128)(2,1)} %param.15), kind=kLoop, calls=%fused_computation.31 | loop fusion | flops 1179136 | bytes 2363392 | tf_op jit(solution)/shard_map/transpose(jvp())/reduce_sum | solution.py:44
  5.3 71.6 %gather_all.1 = (bf16[3,4,256,512]{3,2,1,0:T(8,128)(2,1)S(1)}, bf16[4,512,384]{2,1,0:T(8,128)(2,1)S(1)}, bf16[512,512]{1,0:T(8,128)(2,1)S(1)}, bf16[512,2048]{1,...) custom-call(s32[256]{0:T(256)S(1)} %fusion.26.inv_ref, ...), custom_call_target="tpu_custom_call" | custom-call | tf_op jit(solution)/shard_map/gather_all/pallas_call | solution.py:729
  76.9 1.7 copy-done
  78.6 1.3 copy-done.7
  79.9 1.4 copy-done.9
  81.9 29.0 %attend.1 = (bf16[3,1024,384]{2,1,0:T(8,128)(2,1)S(1)}, bf16[4,3,256,128]{3,2,1,0:T(8,128)(2,1)S(1)}, f32[3,8,1024]{2,1,0:T(8,128)S(1)}) custom-call(bf16[3,4,256,512]{3,2,1,0:T(8,128)(2,1)} %copy-done, bf16[512,384]{1,0:T(8,128)(2,1)S(1)} %dynamic-slice_bitcast_fusion.w_ref, f32[1,384]{1,0:T(1,128)S(1)} %broadcast_in_dim.31.b_ref), custom_call_target="tpu_custom_call" | custom-call | tf_op jit(solution)/shard_map/attend/pallas_call | solution.py:151
  111.0 0.6 copy.27
  111.6 0.7 fusion.33
  112.6 0.3 multiply_reduce_fusion.4
  113.3 1.5 copy-done.8
  114.8 3.3 %multiply_convert_fusion = (bf16[768,2048]{1,0:T(8,128)(2,1)S(1)}, f32[768,2048]{1,0:T(8,128)S(1)}) fusion(f32[2048]{0:T(1024)S(1)} %slice.81, bf16[768,512]{1,0:T(8,128)(2,1)S(1)} %fusion.7.yb_ref, bf16[512,2048]{1,0:T(8,128)(2,1)S(1)} %copy-done.8), kind=kOutput, calls=%fused_computation.7 | convolution fusion | flops 1620049920 | bytes 12328960 | tf_op jit(solution)/shard_map/dot_general | solution.py:1064
  118.2 1.6 copy-done.14
  119.8 2.1 fusion.34
  121.9 0.3 multiply_reduce_fusion.3
  122.2 1.0 copy-done.11
  123.3 0.6 fusion.6
  123.9 1.6 fusion.31
  125.7 4.4 %fusion.35 = (bf16[2048]{0:T(1024)(128)(2,1)S(1)}, bf16[768,2048]{1,0:T(8,128)(2,1)S(1)}) fusion(f32[768,2048]{1,0:T(8,128)S(1)} %get-tuple-element.85, f32[2048]{0:T(1024)S(1)} %slice.81, bf16[768,512]{1,0:T(8,128)(2,1)S(1)} %get-tuple-element.60.df_ref, bf16[2048,512]{1,0:T(8,128)(2,1)S(1)} %copy-done.10), kind=kOutput, calls=%fused_computation.89 | convolution fusion | flops 1629485056 | bytes 12333056 | tf_op jit(solution)/shard_map/to,io->ti/dot_general | solution.py:470
  130.1 2.3 multiply_reduce_fusion
  132.4 0.6 fusion.30
  133.0 1.7 fusion.29
  134.7 51.8 %backward.1 = (bf16[192,128,128]{2,1,0:T(8,128)(2,1)}, f32[1,384]{1,0:T(1,128)}, f32[3,256,512]{2,1,0:T(8,128)}) custom-call(bf16[768,512]{1,0:T(8,128)(2,1)} %get-tuple-element.62.da_ref, bf16[512,512]{1,0:T(8,128)(2,1)} %copy-done.5, bf16[4,512,384]{2,1,0:T(8,128)(2,1)} %copy-done.2, f32[3,8,1024]{2,1,0:T(8,128)} %copy-done.6, ...), custom_call_target="tpu_custom_call" | custom-call | tf_op jit(solution)/shard_map/backward/pallas_call | solution.py:365
  186.5 0.7 bitcast_dynamic-update-slice_fusion.1
  187.5 0.7 bitcast_dynamic-update-slice_fusion
  190.0 0.7 copy.30
  190.7 47.4 %scatter_sums.1 = (f32[8,128,128]{2,1,0:T(8,128)}, f32[16,128]{1,0:T(8,128)}) custom-call(s32[256]{0:T(256)} %owner_ref.1, bf16[192,128,128]{2,1,0:T(8,128)(2,1)} %get-tuple-element.41.blocks_ref, bf16[32,16,128]{2,1,0:T(8,128)(2,1)} %bitcast.55), custom_call_target="tpu_custom_call" | custom-call | tf_op jit(solution)/shard_map/scatter_sums/pallas_call | solution.py:958
  238.2 1.3 divide_subtract_fusion
  239.4 5.7 %adam.1 = (f32[8,128,128]{2,1,0:T(8,128)}, f32[8,128,128]{2,1,0:T(8,128)}, f32[8,128,128]{2,1,0:T(8,128)}, bf16[8,128,128]{2,1,0:T(8,128)(2,1)}, f32[8,128,128]{2,1,0:T(8,128)}) custom-call(f32[8,128,128]{2,1,0:T(8,128)} %get-tuple-element.105.grad_ref, f32[8,128,128]{2,1,0:T(8,128)} %master_ref.1, f32[8,128,128]{2,1,0:T(8,128)} %one_ref.1, ...), custom_call_target="tpu_custom_call" | custom-call | tf_op jit(solution)/shard_map/adam/pallas_call | solution.py:459
  245.1 1.1 copy.52
  246.5 0.8 copy.53
  (89 shorter events, 4.3 us)
Async XLA Ops:
  0.6 4.4 %copy-start.20 = (s32[256]{0:T(256)S(1)}, s32[256]{0:T(256)}, u32[]{:S(2)}) copy-start(s32[256]{0:T(256)} %owner_ref.1) | copy-start | bytes 3076
  0.7 4.5 %copy-start.19 = (f32[192]{0:T(256)S(1)}, f32[192]{0:T(256)}, u32[]{:S(2)}) copy-start(f32[192]{0:T(256)} %param.25) | copy-start | bytes 2308
  0.7 4.6 %copy-start.16 = (f32[8,128,128]{2,1,0:T(8,128)S(1)}, f32[8,128,128]{2,1,0:T(8,128)}, u32[]{:S(2)}) copy-start(f32[8,128,128]{2,1,0:T(8,128)} %master_ref.1) | copy-start | bytes 1572868
  2.4 2.9 %copy-start.4 = (bf16[3,256,512]{2,1,0:T(8,128)(2,1)S(1)}, bf16[3,256,512]{2,1,0:T(8,128)(2,1)}, u32[]{:S(2)}) copy-start(bf16[3,256,512]{2,1,0:T(8,128)(2,1)} %x_ref.1) | copy-start | bytes 2359300
  76.9 1.7 copy-start
  78.6 1.3 copy-start.7
  79.9 1.4 copy-start.9
  81.3 29.6 %copy-start.2 = (bf16[4,512,384]{2,1,0:T(8,128)(2,1)}, bf16[4,512,384]{2,1,0:T(8,128)(2,1)S(1)}, u32[]{:S(2)}) copy-start(bf16[4,512,384]{2,1,0:T(8,128)(2,1)S(1)} %get-tuple-element.32.w_ref) | copy-start | bytes 4718596
  81.3 30.3 %copy-start.5 = (bf16[512,512]{1,0:T(8,128)(2,1)}, bf16[512,512]{1,0:T(8,128)(2,1)S(1)}, u32[]{:S(2)}) copy-start(bf16[512,512]{1,0:T(8,128)(2,1)S(1)} %get-tuple-element.35.wo_ref) | copy-start | bytes 1572868
  110.9 1.3 copy-start.1
  110.9 1.6 copy-start.3
  111.0 1.7 copy-start.6
  112.9 1.9 copy-start.8
  113.3 4.9 %copy-start.12 = (bf16[768,512]{1,0:T(8,128)(2,1)}, bf16[768,512]{1,0:T(8,128)(2,1)S(1)}, u32[]{:S(2)}) copy-start(bf16[768,512]{1,0:T(8,128)(2,1)S(1)} %fusion.7.yb_ref) | copy-start | bytes 2359300
  114.8 5.0 %copy-start.10 = (bf16[2048,512]{1,0:T(8,128)(2,1)S(1)}, bf16[2048,512]{1,0:T(8,128)(2,1)}, u32[]{:S(2)}) copy-start(bf16[2048,512]{1,0:T(8,128)(2,1)} %copy-done.9) | copy-start | bytes 6291460
  118.2 1.6 copy-start.14
  121.9 1.4 copy-start.11
  125.7 4.4 %copy-start.13 = (bf16[768,512]{1,0:T(8,128)(2,1)}, bf16[768,512]{1,0:T(8,128)(2,1)S(1)}, u32[]{:S(2)}) copy-start(bf16[768,512]{1,0:T(8,128)(2,1)S(1)} %get-tuple-element.60.df_ref) | copy-start | bytes 2359300
  130.1 2.3 copy-start.15
  190.7 47.5 %copy-start.21 = (f32[192]{0:T(256)S(1)}, f32[192]{0:T(256)}, u32[]{:S(2)}) copy-start(f32[192]{0:T(256)} %param.27) | copy-start | bytes 2308
  190.7 47.5 %copy-start.22 = (f32[192]{0:T(256)S(1)}, f32[192]{0:T(256)}, u32[]{:S(2)}) copy-start(f32[192]{0:T(256)} %param.26) | copy-start | bytes 2308
  239.4 5.7 %copy-start.18 = (f32[3,256,512]{2,1,0:T(8,128)S(1)}, f32[3,256,512]{2,1,0:T(8,128)}, u32[]{:S(2)}) copy-start(f32[3,256,512]{2,1,0:T(8,128)} %get-tuple-element.104) | copy-start | bytes 4718596
  245.1 1.4 copy-start.17

commit v2 on v1

--- a/solution.py
+++ b/solution.py
@@ -36,23 +36,6 @@
         pieces.append(vector[offset : offset + extent])
         offset = offset + extent
     return pieces
-
-
-def layer_norm(values, gain, shift):
-    center = values - jnp.mean(values, axis=-1, keepdims=True)
-    spread = jnp.mean(center * center, axis=-1, keepdims=True)
-    return center * lax.rsqrt(spread + NORM_EPS) * gain + shift
-
-
-def gelu_value(values):
-    return 0.5 * values * (1.0 + lax.erf(values * 0.7071067811865476))
-
-
-def gelu_slope(values):
-    return (
-        0.5 * (1.0 + lax.erf(values * 0.7071067811865476))
-        + values * jnp.exp(-0.5 * values * values) * 0.3989422804014327
-    )
 
 
 def span_mask(span_offset, span_len):
@@ -112,66 +95,214 @@
     ]
 
 
+def normalize(values):
+    center = values - jnp.mean(values, axis=-1, keepdims=True)
+    spread = jnp.mean(center * center, axis=-1, keepdims=True)
+    rate = lax.rsqrt(spread + NORM_EPS)
+    return center * rate, rate
+
+
+def normalize_back(grads, hat, rate, gain):
+    scaled = grads * gain
+    mean = jnp.mean(scaled, axis=-1, keepdims=True)
+    along = jnp.mean(scaled * hat, axis=-1, keepdims=True)
+    return rate * (scaled - mean - hat * along)
+
+
+def column_sum(values):
+    return jnp.sum(values, axis=0, keepdims=True)
+
+
 def forward_kernel(
-    x_ref, w_ref, b_ref, qkv_ref, ctx_out, lse_ref, ctx_ref, send_sem, recv_sem, own_sem
+    w_ref,
+    b_ref,
+    wo_ref,
+    up_ref,
+    down_ref,
+    rows_ref,
+    bup_ref,
+    tok_ref,
+    cot_ref,
+    x_any,
+    qkv_out,
+    h_out,
+    du_out,
+    ctx_got,
+    lse_ref,
+    lo_ref,
+    df_ref,
+    yb_ref,
+    da_ref,
+    dz_ref,
+    sums_ref,
+    bup_sum_ref,
+    x_ref,
+    qkv_ref,
+    h_ref,
+    du_ref,
+    slope_ref,
+    first_ref,
+    load_sem,
+    out_sem,
+    ctx_src,
+    ctx_send,
+    ctx_recv,
+    ctx_own,
 ):
-    item = pl.program_id(0)
-
-    @pl.when(item == 0)
-    def _():
-        greet_head(ctx_ref.shape[1])
-
-    head_size, tokens, width = x_ref.shape[0], x_ref.shape[1], x_ref.shape[2]
+    head_size, items, tokens, cols = ctx_got.shape
+    width = wo_ref.shape[0]
+    hidden = up_ref.shape[1]
     length = head_size * tokens
-    cols = w_ref.shape[1] // 3
-    rows = x_ref[...].reshape(length, width)
-    qkv_ref[...] = (contract(rows, w_ref[...], 1, 0) + b_ref[...]).astype(jnp.bfloat16)
+
+    def load(item):
+        return pltpu.make_async_copy(x_any.at[item], x_ref.at[item], load_sem.at[item])
+
+    def save(number, item):
+        source, target = ((qkv_ref, qkv_out), (h_ref, h_out), (du_ref, du_out))[number]
+        return pltpu.make_async_copy(
+            source.at[item], target.at[item], out_sem.at[number, item]
+        )
+
+    def ctx_swap(item):
+        return swap(ctx_src, ctx_got, ctx_send, ctx_recv, ctx_own, item)
+
+    for item in range(items):
+        load(item).start()
+    greet_head(head_size)
     step = min(QUERIES, tokens)
-    for number in range(cols // HD):
-        low = number * HD
-        keys = qkv_ref[:, cols + low : cols + low + HD]
-        values = qkv_ref[:, 2 * cols + low : 2 * cols + low + HD]
-        for begin in range(0, length, step):
-            query = qkv_ref[begin : begin + step, low : low + HD] * jnp.bfloat16(SCALE)
-            scores = contract(keys, query, 1, 1)
-            highest = jnp.max(scores, axis=0, keepdims=True)
-            weights = jnp.exp(scores - highest)
-            summed = jnp.sum(weights, axis=0, keepdims=True)
-            probs = (weights * (1.0 / summed)).astype(jnp.bfloat16)
-            context = contract(values, probs, 0, 0).T.astype(jnp.bfloat16)
-            ctx_ref[item, begin // tokens, pl.ds(begin % tokens, step), low : low + HD] = context
-            lse_ref[number : number + 1, begin : begin + step] = highest + jnp.log(summed)
-    swap_step(ctx_ref, ctx_out, send_sem, recv_sem, own_sem)
-
-
-def attend(inputs_full, weights, bias):
+
+    def attend_item(item, carry):
+        load(item).wait()
+        rows = x_ref[item].reshape(length, width)
+        qkv_ref[item] = (contract(rows, w_ref[...], 1, 0) + b_ref[...]).astype(jnp.bfloat16)
+        save(0, item).start()
+        for number in range(cols // HD):
+            low = number * HD
+            keys = qkv_ref[item, :, cols + low : cols + low + HD]
+            values = qkv_ref[item, :, 2 * cols + low : 2 * cols + low + HD]
+            for begin in range(0, length, step):
+                query = qkv_ref[item, begin : begin + step, low : low + HD] * jnp.bfloat16(SCALE)
+                scores = contract(keys, query, 1, 1)
+                highest = jnp.max(scores, axis=0, keepdims=True)
+                weights = jnp.exp(scores - highest)
+                summed = jnp.sum(weights, axis=0, keepdims=True)
+                probs = (weights * (1.0 / summed)).astype(jnp.bfloat16)
+                context = contract(values, probs, 0, 0).T.astype(jnp.bfloat16)
+                ctx_src[
+                    item, begin // tokens, pl.ds(begin % tokens, step), low : low + HD
+                ] = context
+                lse_ref[item, number : number + 1, begin : begin + step] = highest + jnp.log(
+                    summed
+                )
+        for copy in ctx_swap(item):
+            copy.start()
+        return carry
+
+    lax.fori_loop(0, items, attend_item, 0)
+    sums_ref[...] = jnp.zeros_like(sums_ref)
+    bup_sum_ref[...] = jnp.zeros_like(bup_sum_ref)
+    parts = range(hidden // width)
+
+    def layer_item(item, carry):
+        for copy in ctx_swap(item):
+            copy.wait()
+        span = pl.ds(pl.multiple_of(item * tokens, tokens), tokens)
+        z_one = tok_ref[span].astype(jnp.float32) + rows_ref[0:1]
+        for head in range(head_size):
+            z_one = z_one + contract(
+                ctx_got[head, item], wo_ref[head * cols : (head + 1) * cols], 1, 0
+            )
+        hat_one, rate_one = normalize(z_one)
+        first = hat_one * rows_ref[1:2] + rows_ref[2:3]
+        first_ref[...] = first
+        first_low = first.astype(jnp.bfloat16)
+        yb_ref[span] = first_low
+        for part in parts:
+            lanes = slice(part * width, (part + 1) * width)
+            value = contract(first_low, up_ref[:, lanes], 1, 0) + bup_ref[:, lanes]
+            half = 0.5 * (1.0 + lax.erf(value * 0.7071067811865476))
+            h_ref[item, :, lanes] = (value * half).astype(jnp.bfloat16)
+            slope_ref[:, lanes] = (
+                half + value * jnp.exp(-0.5 * value * value) * 0.3989422804014327
+            )
+        save(1, item).start()
+        z_two = first_ref[...] + contract(h_ref[item], down_ref[...], 1, 0) + rows_ref[3:4]
+        hat_two, rate_two = normalize(z_two)
+        lo_ref[span] = (hat_two * rows_ref[4:5] + rows_ref[5:6]).astype(jnp.bfloat16)
+        grads = cot_ref[span].astype(jnp.float32)
+        d_two = normalize_back(grads, hat_two, rate_two, rows_ref[4:5])
+        d_low = d_two.astype(jnp.bfloat16)
+        df_ref[span] = d_low
+        sums_ref[4:5] += column_sum(d_low.astype(jnp.float32))
+        sums_ref[5:6] += column_sum(grads * hat_two)
+        sums_ref[6:7] += column_sum(grads)
+        d_first = d_two
+        for part in parts:
+            lanes = slice(part * width, (part + 1) * width)
+            value = contract(d_low, down_ref[lanes], 1, 1) * slope_ref[:, lanes]
+            short = value.astype(jnp.bfloat16)
+            du_ref[item, :, lanes] = short
+            bup_sum_ref[:, lanes] += column_sum(short.astype(jnp.float32))
+        save(2, item).start()
+        d_first = d_first + contract(du_ref[item], up_ref[...], 1, 1)
+        d_one = normalize_back(d_first, hat_one, rate_one, rows_ref[1:2])
+        dz_ref[span] = d_one
+        short = d_one.astype(jnp.bfloat16)
+        da_ref[span] = short
+        sums_ref[0:1] += column_sum(short.astype(jnp.float32))
+        sums_ref[1:2] += column_sum(d_first * hat_one)
+        sums_ref[2:3] += column_sum(d_first)
+        return carry
+
+    lax.fori_loop(0, items, layer_item, 0)
+    for number in range(3):
+        for item in range(items):
+            save(number, item).wait()
+
+
+def forward_all(w_own, b_own, w_out, w_up, w_down, rows, b_up, token_rows, masked, inputs_full):
     seq_local, head_size, tokens, width = inputs_full.shape
     length = head_size * tokens
-    cols = weights.shape[1] // 3
+    cols = w_own.shape[1] // 3
+    hidden = w_up.shape[1]
+    own = seq_local * tokens
+    short = jnp.bfloat16
+    whole = pl.BlockSpec(memory_space=pltpu.VMEM)
+    any_space = pl.BlockSpec(memory_space=pl.ANY)
     return pl.pallas_call(
         forward_kernel,
-        grid=(seq_local,),
         out_shape=(
-            jax.ShapeDtypeStruct((seq_local, length, 3 * cols), jnp.bfloat16),
-            jax.ShapeDtypeStruct((head_size, seq_local, tokens, cols), jnp.bfloat16),
+            jax.ShapeDtypeStruct((seq_local, length, 3 * cols), short),
+            jax.ShapeDtypeStruct((seq_local, tokens, hidden), short),
+            jax.ShapeDtypeStruct((seq_local, tokens, hidden), short),
+            jax.ShapeDtypeStruct((head_size, seq_local, tokens, cols), short),
             jax.ShapeDtypeStruct((seq_local, 8, length), jnp.float32),
+            jax.ShapeDtypeStruct((own, width), short),
+            jax.ShapeDtypeStruct((own, width), short),
+            jax.ShapeDtypeStruct((own, width), short),
+            jax.ShapeDtypeStruct((own, width), short),
+            jax.ShapeDtypeStruct((own, width), jnp.float32),
+            jax.ShapeDtypeStruct((8, width), jnp.float32),
+            jax.ShapeDtypeStruct((1, hidden), jnp.float32),
         ),
-        in_specs=[
-            pl.BlockSpec((None, head_size, tokens, width), lambda s: (s, 0, 0, 0)),
-            pl.BlockSpec((width, 3 * cols), lambda s: (0, 0)),
-            pl.BlockSpec((1, 3 * cols), lambda s: (0, 0)),
-        ],
-        out_specs=(
-            pl.BlockSpec((None, length, 3 * cols), lambda s: (s, 0, 0)),
-            pl.BlockSpec(memory_space=pl.ANY),
-            pl.BlockSpec((None, 8, length), lambda s: (s, 0, 0)),
+        in_specs=[whole] * 9 + [any_space],
+        out_specs=(any_space,) * 3 + (whole,) * 9,
+        scratch_shapes=[
+            pltpu.VMEM(inputs_full.shape, short),
+            pltpu.VMEM((seq_local, length, 3 * cols), short),
+            pltpu.VMEM((seq_local, tokens, hidden), short),
+            pltpu.VMEM((seq_local, tokens, hidden), short),
+            pltpu.VMEM((tokens, hidden), jnp.float32),
+            pltpu.VMEM((tokens, width), jnp.float32),
+            pltpu.SemaphoreType.DMA((seq_local,)),
+            pltpu.SemaphoreType.DMA((3, seq_local)),
+        ]
+        + swap_scratch(seq_local, head_size, tokens, cols),
+        compiler_params=pltpu.CompilerParams(
+            collective_id=2, has_side_effects=True, vmem_limit_bytes=60 * 1024 * 1024
         ),
-        scratch_shapes=swap_scratch(seq_local, head_size, tokens, cols),
-        compiler_params=pltpu.CompilerParams(
-            collective_id=2, has_side_effects=True, vmem_limit_bytes=48 * 1024 * 1024
-        ),
-        name="attend",
-    )(inputs_full, weights, bias)
+        name="forward_all",
+    )(w_own, b_own, w_out, w_up, w_down, rows, b_up, token_rows, masked, inputs_full)
 
 
 def backward_kernel(
@@ -466,10 +597,6 @@
     )(grads, master, moment_one, moment_two, basis_left, basis_right, average)
 
 
-def back_product(grads, weight):
-    return jnp.einsum("to,io->ti", grads, weight, preferred_element_type=jnp.float32)
-
-
 MESH = pl.DeviceIdType.MESH
 VEC_ROWS = 16
 PIECE = 16
@@ -1018,6 +1145,10 @@
 
     dims = cut(seq_size, head_size)
 
+    mask = span_mask(span_offset, span_len)
+    masked = jnp.where(mask[:, :, None] > 0, cotangent, jnp.zeros_like(cotangent))
+    masked = masked.reshape(seq_local * tok_local, width)
+
     packed = jnp.concatenate(
         [
             master.astype(jnp.bfloat16).reshape(slots_local * BLK, BLK),
@@ -1055,34 +1186,35 @@
 
     w_own = lax.dynamic_index_in_dim(w_qkv, head_index, 0, keepdims=False)
     b_own = jnp.concatenate([own(b_query), jnp.zeros((cols,), jnp.float32), own(b_value)], 0)
-    qkv, context, log_total = attend(inputs_full, w_own, b_own[None, :])
-    context_rows = context.transpose(1, 2, 0, 3).reshape(seq_local * tok_local, width)
-    branch = jnp.dot(context_rows, w_out, preferred_element_type=jnp.float32) + b_out
-    z_one = token_rows.astype(jnp.float32) + branch
-    first = layer_norm(z_one, gain_one, shift_one)
-    first_low = first.astype(jnp.bfloat16)
-    hidden_in = jnp.dot(first_low, w_up, preferred_element_type=jnp.float32) + b_up
-    hidden_act = gelu_value(hidden_in).astype(jnp.bfloat16)
-    ffn_out = jnp.dot(hidden_act, w_down, preferred_element_type=jnp.float32) + b_down
-    z_two = first + ffn_out
-    result, pull_two = jax.vjp(layer_norm, z_two, gain_two, shift_two)
-    layer_out = result.astype(jnp.bfloat16).reshape(local_shape)
-    mask = span_mask(span_offset, span_len)
-    grad_out = (cotangent.astype(jnp.float32) * mask[:, :, None]).reshape(
-        seq_local * tok_local, width
-    )
-    d_ztwo, d_gain_two, d_shift_two = pull_two(grad_out)
-    d_ffn = d_ztwo.astype(jnp.bfloat16)
-    grad_bdown = jnp.sum(d_ffn.astype(jnp.float32), axis=0)
-    d_hidden = back_product(d_ffn, w_down)
-    d_hidden_in = (d_hidden * gelu_slope(hidden_in)).astype(jnp.bfloat16)
-    grad_bup = jnp.sum(d_hidden_in.astype(jnp.float32), axis=0)
-    d_first = d_ztwo + back_product(d_hidden_in, w_up)
-    sink, pull_one = jax.vjp(layer_norm, z_one, gain_one, shift_one)
-    d_zone, d_gain_one, d_shift_one = pull_one(d_first)
-    d_branch = d_zone.astype(jnp.bfloat16)
-    grad_bout = jnp.sum(d_branch.astype(jnp.float32), axis=0)
-
+    rows = jnp.stack(
+        [b_out, gain_one, shift_one, b_down, gain_two, shift_two, b_down, b_down], 0
+    )
+    (
+        qkv,
+        hidden_act,
+        d_hidden_in,
+        context,
+        log_total,
+        layer_out,
+        d_ffn,
+        first_low,
+        d_branch,
+        d_zone,
+        sums,
+        grad_bup,
+    ) = forward_all(
+        w_own,
+        b_own[None, :],
+        w_out,
+        w_up,
+        w_down,
+        rows,
+        b_up[None, :],
+        token_rows,
+        masked,
+        inputs_full,
+    )
+    layer_out = layer_out.reshape(local_shape)
     blocks, grad_b_own, input_grad = backward(
         d_branch,
         w_out,
@@ -1092,8 +1224,8 @@
         d_ffn,
         first_low,
         context,
-        hidden_act,
-        d_hidden_in,
+        hidden_act.reshape(seq_local * tok_local, FF),
+        d_hidden_in.reshape(seq_local * tok_local, FF),
         inputs_full,
         qkv,
     )
@@ -1107,13 +1239,9 @@
         [
             put(grad_b_own[:cols]),
             put(grad_b_own[2 * cols :]),
-            grad_bout,
-            d_gain_one,
-            d_shift_one,
-            grad_bup,
-            grad_bdown,
-            d_gain_two,
-            d_shift_two,
+            sums[0:3].reshape(-1),
+            grad_bup.reshape(-1),
+            sums[4:7].reshape(-1),
         ],
         0,
     ).reshape(total, vec_local)

time: 252 us -> 244 us (0.968)
  Pallas kernels: 205 us -> 218 us
  matrix products: 12.7 us -> 0 us
  other arithmetic: 9.95 us -> 5.28 us
    dot_general x5 -> x0, matrix products: 12.7 us -> none  [the longest x2 6.68 us: back_product(): jnp.einsum('to,io->ti', grads, weight, preferred_element_type=jnp.float32)]
    pallas_call x1, Pallas kernels: 29 us -> 41.5 us  [forward_all(): pl.pallas_call(forward_kernel, out_shape=(jax.ShapeDtypeStruct((seq_local...]
    reduce_sum x8 -> x0, other arithmetic: 7.88 us -> none  [the longest x2 3.16 us: layer_norm(): return center * lax.rsqrt(spread + NORM_EPS) * gain + shift]
    unnamed x59 -> x44, local copies, waits for them, and re-layouts: 13.6 us -> 10.9 us
where the time goes in v2:
time: 244 us; the launch traced here: 240 us
  Pallas kernels  218 us (89%)
  local copies, waits for them, and re-layouts  16.2 us (7%)
  other arithmetic  5.28 us (2%)
    pallas_call x1, Pallas kernels, gather_all(): pl.pallas_call(functools.partial(gather_kernel, dims), out_shape=(jax.Sha...  71.5 us
    pallas_call x1, Pallas kernels, backward(): pl.pallas_call(backward_kernel, out_shape=(jax.ShapeDtypeStruct((NBLK, BL...  51.6 us
    pallas_call x1, Pallas kernels, scatter_sums(): pl.pallas_call(functools.partial(scatter_kernel, dims, slots), out_shape=...  47.5 us
    pallas_call x1, Pallas kernels, forward_all(): pl.pallas_call(forward_kernel, out_shape=(jax.ShapeDtypeStruct((seq_local...  41.5 us
    unnamed x44, local copies, waits for them, and re-layouts  10.9 us
    pallas_call x1, Pallas kernels, adam(): pl.pallas_call(adam_kernel, grid=(slots // together,), out_shape=(full, f...  5.72 us

profile of v2, /device:TPU:11, one launch (start us, length us, event | category | flops | bytes accessed | tf_op | source)
XLA Modules:
  0.0 240.2 jit_solution(4974658084628565788)
XLA Ops:
  0.7 0.7 reduce-precision_convert_fusion.1
  1.4 1.2 convert_element_type.30
  2.6 0.8 select_reduce_fusion
  3.5 1.1 copy-done.1
  4.6 71.5 %gather_all.1 = (bf16[3,4,256,512]{3,2,1,0:T(8,128)(2,1)S(1)}, bf16[4,512,384]{2,1,0:T(8,128)(2,1)S(1)}, bf16[512,512]{1,0:T(8,128)(2,1)S(1)}, bf16[512,2048]{1,...) custom-call(s32[256]{0:T(256)S(1)} %fusion.12.inv_ref, ...), custom_call_target="tpu_custom_call" | custom-call | tf_op jit(solution)/shard_map/gather_all/pallas_call | solution.py:856
  76.1 1.7 copy-done
  77.8 0.8 copy-done.3
  78.6 1.3 copy-done.4
  80.0 1.3 copy-done.5
  81.3 0.1 reshape.160
  81.5 0.1 fusion
  81.7 0.7 stack.29.rows_ref
  82.6 0.6 broadcast_in_dim.46.b_ref
  83.1 0.8 dynamic-slice_bitcast_fusion.w_ref
  83.9 0.6 slice.94
  84.9 1.1 broadcast_select_fusion
  85.9 41.5 %forward_all.1 = (bf16[3,1024,384]{2,1,0:T(8,128)(2,1)}, bf16[3,256,2048]{2,1,0:T(8,128)(2,1)}, bf16[3,256,2048]{2,1,0:T(8,128)(2,1)}, bf16[4,3,256,128]{3,2,1,0...) custom-call(bf16[512,384]{1,0:T(8,128)(2,1)} %dynamic-slice_bitcast_, ...), custom_call_target="tpu_custom_call" | custom-call | tf_op jit(solution)/shard_map/forward_all/pallas_call | solution.py:272
  127.5 51.6 %backward.1 = (bf16[192,128,128]{2,1,0:T(8,128)(2,1)}, f32[1,384]{1,0:T(1,128)}, f32[3,256,512]{2,1,0:T(8,128)}) custom-call(bf16[768,512]{1,0:T(8,128)(2,1)} %get-tuple-element.47.da_ref, bf16[512,512]{1,0:T(8,128)(2,1)} %copy-done.3, bf16[4,512,384]{2,1,0:T(8,128)(2,1)} %copy-done.2, f32[3,8,1024]{2,1,0:T(8,128)} %get-tuple-element.48.lse_ref, ...), custom_call_target="tpu_custom_call" | custom-call | tf_op jit(solution)/shard_map/backward/pallas_call | solution.py:496
  179.1 0.8 bitcast_dynamic-update-slice_fusion.1
  179.8 0.2 dynamic-update-slice
  180.1 0.8 bitcast_dynamic-update-slice_fusion
  180.8 0.2 dynamic-update-slice.1
  181.1 0.3 dynamic-update-slice.2
  181.4 0.3 dynamic-update-slice.3
  181.7 0.3 dynamic-update-slice.4
  182.1 0.7 copy.27
  182.8 47.5 %scatter_sums.1 = (f32[8,128,128]{2,1,0:T(8,128)}, f32[16,128]{1,0:T(8,128)}) custom-call(s32[256]{0:T(256)} %owner_ref.1, bf16[192,128,128]{2,1,0:T(8,128)(2,1)} %get-tuple-element.57.blocks_ref, bf16[32,16,128]{2,1,0:T(8,128)(2,1)} %bitcast.38), custom_call_target="tpu_custom_call" | custom-call | tf_op jit(solution)/shard_map/scatter_sums/pallas_call | solution.py:1085
  230.4 5.7 %adam.1 = (f32[8,128,128]{2,1,0:T(8,128)}, f32[8,128,128]{2,1,0:T(8,128)}, f32[8,128,128]{2,1,0:T(8,128)}, bf16[8,128,128]{2,1,0:T(8,128)(2,1)}, f32[8,128,128]{2,1,0:T(8,128)}) custom-call(f32[8,128,128]{2,1,0:T(8,128)} %get-tuple-element.99.grad_ref, f32[8,128,128]{2,1,0:T(8,128)} %master_ref.1, f32[8,128,128]{2,1,0:T(8,128)} %one_ref.1, ...), custom_call_target="tpu_custom_call" | custom-call | tf_op jit(solution)/shard_map/adam/pallas_call | solution.py:590
  236.1 1.3 divide_subtract_fusion
  237.4 0.9 copy.40
  238.3 1.1 copy.41
  239.4 0.8 copy.42
  (58 shorter events, 1.0 us)
Async XLA Ops:
  0.6 83.9 %copy-start.13 = (s32[3,16]{1,0:T(4,128)S(1)}, s32[3,16]{1,0:T(4,128)}, u32[]{:S(2)}) copy-start(s32[3,16]{1,0:T(4,128)} %param.16) | copy-start | bytes 580
  0.7 84.0 %copy-start.14 = (s32[3,16]{1,0:T(4,128)S(1)}, s32[3,16]{1,0:T(4,128)}, u32[]{:S(2)}) copy-start(s32[3,16]{1,0:T(4,128)} %param.17) | copy-start | bytes 580
  1.4 83.4 %copy-start.9 = (bf16[3,256,512]{2,1,0:T(8,128)(2,1)S(1)}, bf16[3,256,512]{2,1,0:T(8,128)(2,1)}, u32[]{:S(2)}) copy-start(bf16[3,256,512]{2,1,0:T(8,128)(2,1)} %param.15) | copy-start | bytes 2359300
  3.4 1.1 copy-start.1
  76.1 1.7 copy-start
  77.8 0.8 copy-start.3
  78.6 1.3 copy-start.4
  80.0 1.3 copy-start.5
  81.3 46.1 %copy-start.2 = (bf16[4,512,384]{2,1,0:T(8,128)(2,1)}, bf16[4,512,384]{2,1,0:T(8,128)(2,1)S(1)}, u32[]{:S(2)}) copy-start(bf16[4,512,384]{2,1,0:T(8,128)(2,1)S(1)} %get-tuple-element.40.w_ref) | copy-start | bytes 4718596
  127.4 53.6 %copy-start.10 = (f32[8,512]{1,0:T(8,128)S(1)}, f32[8,512]{1,0:T(8,128)}, u32[]{:S(2)}) copy-start(f32[8,512]{1,0:T(8,128)} %get-tuple-element.59) | copy-start | bytes 49156
  127.4 54.0 %copy-start.11 = (f32[1,2048]{1,0:T(1,128)S(1)}, f32[1,2048]{1,0:T(1,128)}, u32[]{:S(2)}) copy-start(f32[1,2048]{1,0:T(1,128)} %get-tuple-element.60) | copy-start | bytes 24580
  230.3 5.8 %copy-start.12 = (f32[192]{0:T(256)S(1)}, f32[192]{0:T(256)}, u32[]{:S(2)}) copy-start(f32[192]{0:T(256)} %param.25) | copy-start | bytes 2308
  230.3 5.8 %copy-start.15 = (f32[192]{0:T(256)S(1)}, f32[192]{0:T(256)}, u32[]{:S(2)}) copy-start(f32[192]{0:T(256)} %param.27) | copy-start | bytes 2308
  230.3 5.8 %copy-start.16 = (f32[192]{0:T(256)S(1)}, f32[192]{0:T(256)}, u32[]{:S(2)}) copy-start(f32[192]{0:T(256)} %param.26) | copy-start | bytes 2308
  230.4 7.0 %copy-start.8 = (bf16[768,512]{1,0:T(8,128)(2,1)S(1)}, bf16[768,512]{1,0:T(8,128)(2,1)}, u32[]{:S(2)}) copy-start(bf16[768,512]{1,0:T(8,128)(2,1)} %get-tuple-element.46) | copy-start | bytes 2359300
  230.4 7.9 %copy-start.7 = (f32[3,256,512]{2,1,0:T(8,128)S(1)}, f32[3,256,512]{2,1,0:T(8,128)}, u32[]{:S(2)}) copy-start(f32[3,256,512]{2,1,0:T(8,128)} %get-tuple-element.98) | copy-start | bytes 4718596
  237.4 2.0 copy-start.6

commit v3 on v2

--- a/solution.py
+++ b/solution.py
@@ -368,6 +368,8 @@
         for copy in dctx_swap(item):
             copy.start()
 
+    blocks_ref[NBLK] = jnp.zeros((BLK, BLK), jnp.bfloat16)
+
     first = 3 * across * across
     for head in range(head_size):
         value = contract(ctx_ref[head].reshape(items * tokens, cols), da_ref[...], 0, 0)
@@ -496,7 +498,7 @@
     return pl.pallas_call(
         backward_kernel,
         out_shape=(
-            jax.ShapeDtypeStruct((NBLK, BLK, BLK), jnp.bfloat16),
+            jax.ShapeDtypeStruct((NBLK + 1, BLK, BLK), jnp.bfloat16),
             jax.ShapeDtypeStruct((1, 3 * cols), jnp.float32),
             jax.ShapeDtypeStruct((seq_local, tokens, width), jnp.float32),
         ),
@@ -693,10 +695,9 @@
     own_x.start()
     own_w.start()
     greet(dims, me)
-    started = []
-
-    def send_x(source, head, target, number):
-        copy = pltpu.make_async_remote_copy(
+
+    def copy_x(source, head, target, number):
+        return pltpu.make_async_remote_copy(
             src_ref=source,
             dst_ref=xf_ref.at[:, head],
             send_sem=x_send.at[number],
@@ -704,8 +705,10 @@
             device_id=device(dims, target),
             device_id_type=MESH,
         )
+
+    def send_x(source, head, target, number):
+        copy = copy_x(source, head, target, number)
         copy.start()
-        started.append(copy)
 
     def arrived_x(head):
         pltpu.make_async_remote_copy(
@@ -717,74 +720,122 @@
             device_id_type=MESH,
         ).wait_recv()
 
-    count = [0]
-
-    def send_w(source, index, target):
-        number = count[0]
-        count[0] = number + 1
-        copy = pltpu.make_async_remote_copy(
-            src_ref=source,
-            dst_ref=spot(index),
-            send_sem=w_send.at[number],
-            recv_sem=w_recv.at[index],
-            device_id=device(dims, target),
-            device_id_type=MESH,
-        )
-        copy.start()
-        started.append(copy)
-
-    def arrived_w(index):
-        pltpu.make_async_remote_copy(
-            src_ref=w_ref,
-            dst_ref=spot(index),
-            send_sem=w_send.at[0],
-            recv_sem=w_recv.at[index],
-            device_id=device(dims, me),
-            device_id_type=MESH,
-        ).wait_recv()
-
-    order = [0, 2, 1, 3]
-
-    def forward(source, coords, after):
-        for axis in order[after:]:
+    def first_x():
+        number = 0
+        for step in range(1, size_y):
+            send_x(x_ref, head_me, moved(dims, me, 2, step), number)
+            number = number + 1
+        for step in range(1, size_c):
+            send_x(x_ref, head_me, moved(dims, me, 3, step), number)
+            number = number + 1
+
+    def pass_x():
+        number = size_y + size_c - 2
+        for step in range(1, size_y):
+            other = moved(dims, me, 2, step)
+            head = other[2] * size_c + other[3]
+            arrived_x(head)
+            for hop in range(1, size_c):
+                send_x(xf_ref.at[:, head], head, moved(dims, me, 3, hop), number)
+                number = number + 1
+
+    def end_x():
+        for number in range((size_y - 1) * size_c + size_c - 1):
+            copy_x(x_ref, head_me, moved(dims, me, 3, 1), number).wait_send()
+
+    def run(order):
+        sent = []
+
+        def when(condition, action):
+            if condition is None:
+                action()
+            else:
+                pl.when(condition)(action)
+
+        def both(one, other):
+            if one is None or other is None:
+                return other if one is None else one
+            return jnp.logical_and(one, other)
+
+        def send(source, coords, target, condition):
+            index = flat(dims, coords)
+            copy = pltpu.make_async_remote_copy(
+                src_ref=source,
+                dst_ref=spot(index),
+                send_sem=w_send.at[len(sent)],
+                recv_sem=w_recv.at[index],
+                device_id=device(dims, target),
+                device_id_type=MESH,
+            )
+            when(condition, copy.start)
+            sent.append((condition, copy.wait_send))
+
+        def along(source, coords, direction, condition):
+            target = (lax.rem(me[0] + direction + size_z, size_z),) + tuple(me[1:])
+            inside = me[0] < size_z - 1 if direction > 0 else me[0] > 0
+            send(source, coords, target, both(condition, inside))
+
+        def forward(source, coords, later, condition=None):
+            for axis in later:
+                if axis == 0:
+                    along(source, coords, 1, condition)
+                    along(source, coords, -1, condition)
+                    continue
+                for step in range(1, dims[axis]):
+                    send(source, coords, moved(dims, me, axis, step), condition)
+
+        def arrived(coords, condition=None):
+            copy = pltpu.make_async_remote_copy(
+                src_ref=w_ref,
+                dst_ref=spot(flat(dims, coords)),
+                send_sem=w_send.at[0],
+                recv_sem=w_recv.at[flat(dims, coords)],
+                device_id=device(dims, me),
+                device_id_type=MESH,
+            )
+            when(condition, copy.wait_recv)
+
+        forward(w_ref, me, order + [3])
+        first_x()
+        held = [tuple(me)]
+        for level, axis in enumerate(order):
+            later = order[level + 1 :] + [3]
+            fresh = []
             for step in range(1, dims[axis]):
-                send_w(source, flat(dims, coords), moved(dims, me, axis, step))
-
-    number = 0
-    for step in range(1, size_y):
-        send_x(x_ref, head_me, moved(dims, me, 2, step), number)
-        number = number + 1
-    for step in range(1, size_c):
-        send_x(x_ref, head_me, moved(dims, me, 3, step), number)
-        number = number + 1
-    forward(w_ref, me, 0)
-    held = [me]
-    for level in range(3):
-        axis = order[level]
-        fresh = []
-        for step in range(1, dims[axis]):
+                for direction in (1, -1) if axis == 0 else (0,):
+                    for coords in held:
+                        if axis != 0:
+                            source = moved(dims, coords, axis, step)
+                            arrived(source)
+                            forward(spot(flat(dims, source)), source, later)
+                            fresh.append(source)
+                            continue
+                        source = moved(dims, coords, 0, 2 * size_z - direction * step)
+                        there = me[0] >= step if direction > 0 else me[0] < size_z - step
+                        arrived(source, there)
+                        along(spot(flat(dims, source)), source, direction, there)
+                        forward(spot(flat(dims, source)), source, later, there)
+                        if direction > 0:
+                            fresh.append(source)
+            held = held + fresh
+            if level == 1:
+                pass_x()
+        for step in range(1, size_c):
             for coords in held:
-                source = moved(dims, coords, axis, step)
-                arrived_w(flat(dims, source))
-                forward(spot(flat(dims, source)), source, level + 1)
-                fresh.append(source)
-        held = held + fresh
-        if level == 1:
-            for step in range(1, size_y):
-                other = moved(dims, me, 2, step)
-                head = other[2] * size_c + other[3]
-                arrived_x(head)
-                for hop in range(1, size_c):
-                    send_x(xf_ref.at[:, head], head, moved(dims, me, 3, hop), number)
-                    number = number + 1
-    for step in range(1, size_c):
-        for coords in held:
-            arrived_w(flat(dims, moved(dims, coords, 3, step)))
-        for across in range(size_y):
-            other = moved(dims, moved(dims, me, 3, step), 2, across)
-            arrived_x(other[2] * size_c + other[3])
-    for copy in started:
-        copy.wait_send()
+                arrived(moved(dims, coords, 3, step))
+            for across in range(size_y):
+                other = moved(dims, moved(dims, me, 3, step), 2, across)
+                arrived_x(other[2] * size_c + other[3])
+        for condition, wait in sent:
+            when(condition, wait)
+        end_x()
+
+    for core in range(size_c):
+
+        @pl.when(me[3] == core)
+        def _(core=core):
+            run([2, 0, 1] if core % 2 == 0 else [2, 1, 0])
+
     own_x.wait()
     own_w.wait()
     unpack(dims, inv_ref, wf_ref, qkv_ref, out_ref, up_ref, down_ref)
@@ -847,12 +898,7 @@
     any_space = pl.BlockSpec(memory_space=pl.ANY)
     whole = pl.BlockSpec(memory_space=pltpu.VMEM)
     sends_x = (size_y - 1) * size_c + size_c - 1
-    sends_w = (
-        (size_z - 1)
-        + size_z * (size_y - 1)
-        + size_z * size_y * (size_x - 1)
-        + size_z * size_y * size_x * (size_c - 1)
-    )
+    sends_w = 3 * total
     return pl.pallas_call(
         functools.partial(gather_kernel, dims),
         out_shape=(
@@ -908,33 +954,33 @@
     greet(dims, me)
 
     def block_of(dest, slot):
-        owner = owner_ref[dest * slots + slot]
-        block = blocks_ref[jnp.minimum(owner, NBLK - 1)]
-        return jnp.where(owner < NBLK, block, jnp.zeros_like(block))
-
-    def total_of(dest, extras, keep_block, keep_vec):
+        return blocks_ref[jnp.minimum(owner_ref[dest * slots + slot], NBLK)]
+
+    def total_of(dest, extras, keep_block, keep_vec, kind=jnp.float32):
         def one(slot, carry):
-            value = block_of(dest, slot).astype(jnp.float32)
+            value = block_of(dest, slot).astype(kind)
             span = pl.ds(pl.multiple_of(slot * BLK, BLK), BLK)
             for ref, lead in extras:
-                value = value + ref[lead + (span,)].astype(jnp.float32)
+                value = value + ref[lead + (span,)].astype(kind)
             keep_block(slot, span, value)
             return carry
 
         lax.fori_loop(0, slots, one, 0)
-        value = vec_ref[dest].astype(jnp.float32)
+        value = vec_ref[dest].astype(kind)
         for ref, lead in extras:
-            value = value + ref[lead + (pl.ds(rows, VEC_ROWS),)].astype(jnp.float32)
+            value = value + ref[lead + (pl.ds(rows, VEC_ROWS),)].astype(kind)
         keep_vec(value)
 
     def into_term(dest, extras):
+        narrow = len(extras) < 2
+
         def keep_block(slot, span, value):
             term[dest, span] = value.astype(jnp.bfloat16)
 
         def keep_vec(value):
             term[dest, pl.ds(rows, VEC_ROWS)] = value.astype(jnp.bfloat16)
 
-        total_of(dest, extras, keep_block, keep_vec)
+        total_of(dest, extras, keep_block, keep_vec, jnp.bfloat16 if narrow else jnp.float32)
 
     def remote(dest, got, send, recv, hop, index, target):
         return pltpu.make_async_remote_copy(

time: 244 us -> 233 us (0.955)
  Pallas kernels: 218 us -> 207 us
    pallas_call x1, Pallas kernels: 71.5 us -> 59.2 us  [gather_all(): pl.pallas_call(functools.partial(gather_kernel, dims), out_shape=(jax.Sha...]
where the time goes in v3:
time: 233 us; the launch traced here: 229 us
  Pallas kernels  207 us (89%)
  local copies, waits for them, and re-layouts  16.1 us (7%)
  other arithmetic  5.29 us (2%)
    pallas_call x1, Pallas kernels, gather_all(): pl.pallas_call(functools.partial(gather_kernel, dims), out_shape=(jax.Sha...  59.2 us
    pallas_call x1, Pallas kernels, backward(): pl.pallas_call(backward_kernel, out_shape=(jax.ShapeDtypeStruct((NBLK + 1...  51.1 us
    pallas_call x1, Pallas kernels, scatter_sums(): pl.pallas_call(functools.partial(scatter_kernel, dims, slots), out_shape=...  49.5 us
    pallas_call x1, Pallas kernels, forward_all(): pl.pallas_call(forward_kernel, out_shape=(jax.ShapeDtypeStruct((seq_local...  41.4 us
    unnamed x44, local copies, waits for them, and re-layouts  10.9 us
    pallas_call x1, Pallas kernels, adam(): pl.pallas_call(adam_kernel, grid=(slots // together,), out_shape=(full, f...  5.71 us

profile of v3, /device:TPU:11, one launch (start us, length us, event | category | flops | bytes accessed | tf_op | source)
XLA Modules:
  0.0 229.2 jit_solution(2081431033567013382)
XLA Ops:
  0.7 0.7 reduce-precision_convert_fusion.1
  1.4 1.2 convert_element_type.30
  2.6 0.8 select_reduce_fusion
  3.5 1.1 copy-done.1
  4.6 59.2 %gather_all.1 = (bf16[3,4,256,512]{3,2,1,0:T(8,128)(2,1)S(1)}, bf16[4,512,384]{2,1,0:T(8,128)(2,1)S(1)}, bf16[512,512]{1,0:T(8,128)(2,1)S(1)}, bf16[512,2048]{1,...) custom-call(s32[256]{0:T(256)S(1)} %fusion.12.inv_ref, ...), custom_call_target="tpu_custom_call" | custom-call | tf_op jit(solution)/shard_map/gather_all/pallas_call | solution.py:902
  63.8 1.7 copy-done
  65.5 0.8 copy-done.3
  66.3 1.3 copy-done.4
  67.6 1.3 copy-done.5
  69.0 0.1 reshape.160
  69.1 0.1 fusion
  69.3 0.7 stack.29.rows_ref
  70.2 0.6 broadcast_in_dim.46.b_ref
  70.8 0.8 dynamic-slice_bitcast_fusion.w_ref
  71.6 0.6 slice.94
  72.5 1.1 broadcast_select_fusion
  73.6 41.4 %forward_all.1 = (bf16[3,1024,384]{2,1,0:T(8,128)(2,1)}, bf16[3,256,2048]{2,1,0:T(8,128)(2,1)}, bf16[3,256,2048]{2,1,0:T(8,128)(2,1)}, bf16[4,3,256,128]{3,2,1,0...) custom-call(bf16[512,384]{1,0:T(8,128)(2,1)} %dynamic-slice_bitcast_, ...), custom_call_target="tpu_custom_call" | custom-call | tf_op jit(solution)/shard_map/forward_all/pallas_call | solution.py:272
  115.0 51.1 %backward.1 = (bf16[193,128,128]{2,1,0:T(8,128)(2,1)}, f32[1,384]{1,0:T(1,128)}, f32[3,256,512]{2,1,0:T(8,128)}) custom-call(bf16[768,512]{1,0:T(8,128)(2,1)} %get-tuple-element.47.da_ref, bf16[512,512]{1,0:T(8,128)(2,1)} %copy-done.3, bf16[4,512,384]{2,1,0:T(8,128)(2,1)} %copy-done.2, f32[3,8,1024]{2,1,0:T(8,128)} %get-tuple-element.48.lse_ref, ...), custom_call_target="tpu_custom_call" | custom-call | tf_op jit(solution)/shard_map/backward/pallas_call | solution.py:498
  166.1 0.7 bitcast_dynamic-update-slice_fusion.1
  166.8 0.2 dynamic-update-slice
  167.1 0.7 bitcast_dynamic-update-slice_fusion
  167.8 0.2 dynamic-update-slice.1
  168.0 0.3 dynamic-update-slice.2
  168.4 0.3 dynamic-update-slice.3
  168.7 0.3 dynamic-update-slice.4
  169.0 0.7 copy.27
  169.7 49.5 %scatter_sums.1 = (f32[8,128,128]{2,1,0:T(8,128)}, f32[16,128]{1,0:T(8,128)}) custom-call(s32[256]{0:T(256)} %owner_ref.1, bf16[193,128,128]{2,1,0:T(8,128)(2,1)} %get-tuple-element.57.blocks_ref, bf16[32,16,128]{2,1,0:T(8,128)(2,1)} %bitcast.38), custom_call_target="tpu_custom_call" | custom-call | tf_op jit(solution)/shard_map/scatter_sums/pallas_call | solution.py:1131
  219.3 5.7 %adam.1 = (f32[8,128,128]{2,1,0:T(8,128)}, f32[8,128,128]{2,1,0:T(8,128)}, f32[8,128,128]{2,1,0:T(8,128)}, bf16[8,128,128]{2,1,0:T(8,128)(2,1)}, f32[8,128,128]{2,1,0:T(8,128)}) custom-call(f32[8,128,128]{2,1,0:T(8,128)} %get-tuple-element.99.grad_ref, f32[8,128,128]{2,1,0:T(8,128)} %master_ref.1, f32[8,128,128]{2,1,0:T(8,128)} %one_ref.1, ...), custom_call_target="tpu_custom_call" | custom-call | tf_op jit(solution)/shard_map/adam/pallas_call | solution.py:592
  225.1 1.3 divide_subtract_fusion
  226.3 0.9 copy.40
  227.2 1.1 copy.41
  228.4 0.8 copy.42
  (58 shorter events, 1.0 us)
Async XLA Ops:
  0.6 71.5 %copy-start.13 = (s32[3,16]{1,0:T(4,128)S(1)}, s32[3,16]{1,0:T(4,128)}, u32[]{:S(2)}) copy-start(s32[3,16]{1,0:T(4,128)} %param.16) | copy-start | bytes 580
  0.7 71.7 %copy-start.14 = (s32[3,16]{1,0:T(4,128)S(1)}, s32[3,16]{1,0:T(4,128)}, u32[]{:S(2)}) copy-start(s32[3,16]{1,0:T(4,128)} %param.17) | copy-start | bytes 580
  1.4 71.1 %copy-start.9 = (bf16[3,256,512]{2,1,0:T(8,128)(2,1)S(1)}, bf16[3,256,512]{2,1,0:T(8,128)(2,1)}, u32[]{:S(2)}) copy-start(bf16[3,256,512]{2,1,0:T(8,128)(2,1)} %param.15) | copy-start | bytes 2359300
  3.4 1.1 copy-start.1
  63.8 1.7 copy-start
  65.5 0.8 copy-start.3
  66.3 1.3 copy-start.4
  67.6 1.3 copy-start.5
  68.9 46.0 %copy-start.2 = (bf16[4,512,384]{2,1,0:T(8,128)(2,1)}, bf16[4,512,384]{2,1,0:T(8,128)(2,1)S(1)}, u32[]{:S(2)}) copy-start(bf16[4,512,384]{2,1,0:T(8,128)(2,1)S(1)} %get-tuple-element.40.w_ref) | copy-start | bytes 4718596
  115.0 53.0 %copy-start.10 = (f32[8,512]{1,0:T(8,128)S(1)}, f32[8,512]{1,0:T(8,128)}, u32[]{:S(2)}) copy-start(f32[8,512]{1,0:T(8,128)} %get-tuple-element.59) | copy-start | bytes 49156
  115.0 53.3 %copy-start.11 = (f32[1,2048]{1,0:T(1,128)S(1)}, f32[1,2048]{1,0:T(1,128)}, u32[]{:S(2)}) copy-start(f32[1,2048]{1,0:T(1,128)} %get-tuple-element.60) | copy-start | bytes 24580
  219.3 5.8 %copy-start.12 = (f32[192]{0:T(256)S(1)}, f32[192]{0:T(256)}, u32[]{:S(2)}) copy-start(f32[192]{0:T(256)} %param.25) | copy-start | bytes 2308
  219.3 5.8 %copy-start.15 = (f32[192]{0:T(256)S(1)}, f32[192]{0:T(256)}, u32[]{:S(2)}) copy-start(f32[192]{0:T(256)} %param.27) | copy-start | bytes 2308
  219.3 5.8 %copy-start.16 = (f32[192]{0:T(256)S(1)}, f32[192]{0:T(256)}, u32[]{:S(2)}) copy-start(f32[192]{0:T(256)} %param.26) | copy-start | bytes 2308
  219.3 7.0 %copy-start.8 = (bf16[768,512]{1,0:T(8,128)(2,1)S(1)}, bf16[768,512]{1,0:T(8,128)(2,1)}, u32[]{:S(2)}) copy-start(bf16[768,512]{1,0:T(8,128)(2,1)} %get-tuple-element.46) | copy-start | bytes 2359300
  219.3 7.9 %copy-start.7 = (f32[3,256,512]{2,1,0:T(8,128)S(1)}, f32[3,256,512]{2,1,0:T(8,128)}, u32[]{:S(2)}) copy-start(f32[3,256,512]{2,1,0:T(8,128)} %get-tuple-element.98) | copy-start | bytes 4718596
  226.3 2.0 copy-start.6

commit v4 on v3

--- a/solution.py
+++ b/solution.py
@@ -114,15 +114,15 @@
 
 
 def forward_kernel(
-    w_ref,
     b_ref,
-    wo_ref,
-    up_ref,
-    down_ref,
     rows_ref,
     bup_ref,
     tok_ref,
     cot_ref,
+    w_any,
+    wo_any,
+    up_any,
+    down_any,
     x_any,
     qkv_out,
     h_out,
@@ -142,6 +142,11 @@
     du_ref,
     slope_ref,
     first_ref,
+    w_ref,
+    wo_ref,
+    up_ref,
+    down_ref,
+    weight_sem,
     load_sem,
     out_sem,
     ctx_src,
@@ -166,9 +171,24 @@
     def ctx_swap(item):
         return swap(ctx_src, ctx_got, ctx_send, ctx_recv, ctx_own, item)
 
+    weights = [
+        pltpu.make_async_copy(source, target, weight_sem.at[number])
+        for number, (source, target) in enumerate(
+            [
+                (w_any.at[lax.axis_index("head")], w_ref),
+                (wo_any, wo_ref),
+                (up_any, up_ref),
+                (down_any, down_ref),
+            ]
+        )
+    ]
+    weights[0].start()
     for item in range(items):
         load(item).start()
+    for copy in weights[1:]:
+        copy.start()
     greet_head(head_size)
+    weights[0].wait()
     step = min(QUERIES, tokens)
 
     def attend_item(item, carry):
@@ -199,6 +219,8 @@
         return carry
 
     lax.fori_loop(0, items, attend_item, 0)
+    for copy in weights[1:]:
+        copy.wait()
     sums_ref[...] = jnp.zeros_like(sums_ref)
     bup_sum_ref[...] = jnp.zeros_like(bup_sum_ref)
     parts = range(hidden // width)
@@ -260,10 +282,10 @@
             save(number, item).wait()
 
 
-def forward_all(w_own, b_own, w_out, w_up, w_down, rows, b_up, token_rows, masked, inputs_full):
+def forward_all(b_own, rows, b_up, token_rows, masked, w_qkv, w_out, w_up, w_down, inputs_full):
     seq_local, head_size, tokens, width = inputs_full.shape
     length = head_size * tokens
-    cols = w_own.shape[1] // 3
+    cols = w_qkv.shape[2] // 3
     hidden = w_up.shape[1]
     own = seq_local * tokens
     short = jnp.bfloat16
@@ -285,7 +307,7 @@
             jax.ShapeDtypeStruct((8, width), jnp.float32),
             jax.ShapeDtypeStruct((1, hidden), jnp.float32),
         ),
-        in_specs=[whole] * 9 + [any_space],
+        in_specs=[whole] * 5 + [any_space] * 5,
         out_specs=(any_space,) * 3 + (whole,) * 9,
         scratch_shapes=[
             pltpu.VMEM(inputs_full.shape, short),
@@ -294,6 +316,11 @@
             pltpu.VMEM((seq_local, tokens, hidden), short),
             pltpu.VMEM((tokens, hidden), jnp.float32),
             pltpu.VMEM((tokens, width), jnp.float32),
+            pltpu.VMEM(w_qkv.shape[1:], short),
+            pltpu.VMEM(w_out.shape, short),
+            pltpu.VMEM(w_up.shape, short),
+            pltpu.VMEM(w_down.shape, short),
+            pltpu.SemaphoreType.DMA((4,)),
             pltpu.SemaphoreType.DMA((seq_local,)),
             pltpu.SemaphoreType.DMA((3, seq_local)),
         ]
@@ -302,7 +329,7 @@
             collective_id=2, has_side_effects=True, vmem_limit_bytes=60 * 1024 * 1024
         ),
         name="forward_all",
-    )(w_own, b_own, w_out, w_up, w_down, rows, b_up, token_rows, masked, inputs_full)
+    )(b_own, rows, b_up, token_rows, masked, w_qkv, w_out, w_up, w_down, inputs_full)
 
 
 def backward_kernel(
@@ -834,7 +861,7 @@
 
         @pl.when(me[3] == core)
         def _(core=core):
-            run([2, 0, 1] if core % 2 == 0 else [2, 1, 0])
+            run([2, 0, 1] if core % 2 == 0 else [0, 1, 2])
 
     own_x.wait()
     own_w.wait()
@@ -1230,7 +1257,6 @@
     def own(array):
         return lax.dynamic_slice_in_dim(array, begin, cols, array.ndim - 1)
 
-    w_own = lax.dynamic_index_in_dim(w_qkv, head_index, 0, keepdims=False)
     b_own = jnp.concatenate([own(b_query), jnp.zeros((cols,), jnp.float32), own(b_value)], 0)
     rows = jnp.stack(
         [b_out, gain_one, shift_one, b_down, gain_two, shift_two, b_down, b_down], 0
@@ -1249,15 +1275,15 @@
         sums,
         grad_bup,
     ) = forward_all(
-        w_own,
         b_own[None, :],
-        w_out,
-        w_up,
-        w_down,
         rows,
         b_up[None, :],
         token_rows,
         masked,
+        w_qkv,
+        w_out,
+        w_up,
+        w_down,
         inputs_full,
     )
     layer_out = layer_out.reshape(local_shape)
@@ -1277,9 +1303,10 @@
     )
     grad_b_own = grad_b_own.reshape(-1)
 
+    owned = jnp.arange(width, dtype=jnp.int32) // cols == head_index
+
     def put(array):
-        empty = jnp.zeros(array.shape[:-1] + (width,), array.dtype)
-        return lax.dynamic_update_slice_in_dim(empty, array, begin, array.ndim - 1)
+        return jnp.where(owned, jnp.tile(array, head_size), 0.0)
 
     vector_terms = jnp.concatenate(
         [

time: 233 us -> 225 us (0.966)
  Pallas kernels: 207 us -> 196 us
  other arithmetic: 5.29 us -> 7.88 us
    pallas_call x1, Pallas kernels: 59.2 us -> 51.7 us  [gather_all(): pl.pallas_call(functools.partial(gather_kernel, dims), out_shape=(jax.Sha...]
    unnamed x44 -> x34, local copies, waits for them, and re-layouts: 10.9 us -> 10.8 us
where the time goes in v4:
time: 225 us; the launch traced here: 221 us
  Pallas kernels  196 us (87%)
  local copies, waits for them, and re-layouts  15.7 us (7%)
  other arithmetic  7.88 us (4%)
    pallas_call x1, Pallas kernels, gather_all(): pl.pallas_call(functools.partial(gather_kernel, dims), out_shape=(jax.Sha...  51.7 us
    pallas_call x1, Pallas kernels, backward(): pl.pallas_call(backward_kernel, out_shape=(jax.ShapeDtypeStruct((NBLK + 1...  51.5 us
    pallas_call x1, Pallas kernels, scatter_sums(): pl.pallas_call(functools.partial(scatter_kernel, dims, slots), out_shape=...  47.4 us
    pallas_call x1, Pallas kernels, forward_all(): pl.pallas_call(forward_kernel, out_shape=(jax.ShapeDtypeStruct((seq_local...  40.1 us
    unnamed x34, local copies, waits for them, and re-layouts  10.8 us
    pallas_call x1, Pallas kernels, adam(): pl.pallas_call(adam_kernel, grid=(slots // together,), out_shape=(full, f...  5.66 us

profile of v4, /device:TPU:11, one launch (start us, length us, event | category | flops | bytes accessed | tf_op | source)
XLA Modules:
  0.0 220.8 jit_solution(15987056399536564683)
XLA Ops:
  0.7 0.9 select_reduce_fusion
  1.6 0.7 reduce-precision_convert_fusion.1
  2.3 0.8 broadcast_in_dim.53
  3.2 0.8 broadcast_in_dim.54
  4.0 1.1 convert_element_type.30
  5.1 2.2 broadcast_select_fusion
  7.3 51.7 %gather_all.1 = (bf16[3,4,256,512]{3,2,1,0:T(8,128)(2,1)S(1)}, bf16[4,512,384]{2,1,0:T(8,128)(2,1)S(1)}, bf16[512,512]{1,0:T(8,128)(2,1)S(1)}, bf16[512,2048]{1,...) custom-call(s32[256]{0:T(256)S(1)} %fusion.18.inv_ref, ...), custom_call_target="tpu_custom_call" | custom-call | tf_op jit(solution)/shard_map/gather_all/pallas_call | solution.py:929
  59.1 1.7 copy-done
  60.8 1.1 copy-done.1
  61.9 1.3 copy-done.3
  63.3 1.3 copy-done.4
  64.6 0.8 copy-done.5
  65.8 0.6 slice.88
  66.5 0.6 broadcast_in_dim.51.b_ref
  67.1 0.6 stack.29.rows_ref
  67.7 40.1 %forward_all.1 = (bf16[3,1024,384]{2,1,0:T(8,128)(2,1)}, bf16[3,256,2048]{2,1,0:T(8,128)(2,1)}, bf16[3,256,2048]{2,1,0:T(8,128)(2,1)}, bf16[4,3,256,128]{3,2,1,0...) custom-call(f32[1,384]{1,0:T(1,128)} %broadcast_in_dim.51.b_ref, ...), custom_call_target="tpu_custom_call" | custom-call | tf_op jit(solution)/shard_map/forward_all/pallas_call | solution.py:294
  107.8 0.7 convert_reduce_fusion
  108.5 0.7 convert.24
  109.3 51.5 %backward.1 = (bf16[193,128,128]{2,1,0:T(8,128)(2,1)}, f32[1,384]{1,0:T(1,128)}, f32[3,256,512]{2,1,0:T(8,128)}) custom-call(bf16[768,512]{1,0:T(8,128)(2,1)} %get-tuple-element.47.da_ref, bf16[512,512]{1,0:T(8,128)(2,1)} %copy-done.5, bf16[4,512,384]{2,1,0:T(8,128)(2,1)} %copy-done.1, f32[3,8,1024]{2,1,0:T(8,128)} %get-tuple-element.48.lse_ref, ...), custom_call_target="tpu_custom_call" | custom-call | tf_op jit(solution)/shard_map/backward/pallas_call | solution.py:525
  160.8 0.7 slice_bitcast_fusion
  161.5 0.2 dynamic-update-slice
  161.8 0.2 dynamic-update-slice.1
  162.0 0.3 dynamic-update-slice.2
  162.2 0.3 dynamic-update-slice.3
  162.5 0.2 dynamic-update-slice.4
  162.8 0.7 copy.27
  163.5 47.4 %scatter_sums.1 = (f32[8,128,128]{2,1,0:T(8,128)}, f32[16,128]{1,0:T(8,128)}) custom-call(s32[256]{0:T(256)} %owner_ref.1, bf16[193,128,128]{2,1,0:T(8,128)(2,1)} %get-tuple-element.57.blocks_ref, bf16[32,16,128]{2,1,0:T(8,128)(2,1)} %bitcast.44), custom_call_target="tpu_custom_call" | custom-call | tf_op jit(solution)/shard_map/scatter_sums/pallas_call | solution.py:1158
  211.0 1.3 divide_subtract_fusion
  212.3 5.7 %adam.1 = (f32[8,128,128]{2,1,0:T(8,128)}, f32[8,128,128]{2,1,0:T(8,128)}, f32[8,128,128]{2,1,0:T(8,128)}, bf16[8,128,128]{2,1,0:T(8,128)(2,1)}, f32[8,128,128]{2,1,0:T(8,128)}) custom-call(f32[8,128,128]{2,1,0:T(8,128)} %get-tuple-element.103.grad_ref, f32[8,128,128]{2,1,0:T(8,128)} %master_ref.1, f32[8,128,128]{2,1,0:T(8,128)} %one_ref.1, ...), custom_call_target="tpu_custom_call" | custom-call | tf_op jit(solution)/shard_map/adam/pallas_call | solution.py:619
  218.0 0.9 copy.38
  218.8 1.1 copy.39
  220.0 0.8 copy.40
  (43 shorter events, 1.0 us)
Async XLA Ops:
  0.6 6.7 %copy-start.2 = (bf16[3,256,512]{2,1,0:T(8,128)(2,1)S(1)}, bf16[3,256,512]{2,1,0:T(8,128)(2,1)}, u32[]{:S(2)}) copy-start(bf16[3,256,512]{2,1,0:T(8,128)(2,1)} %x_ref.1) | copy-start | bytes 2359300
  59.1 1.7 copy-start
  60.8 1.1 copy-start.1
  61.9 1.3 copy-start.3
  63.3 1.3 copy-start.4
  64.6 0.8 copy-start.5
  163.5 47.4 %copy-start.9 = (f32[192]{0:T(256)S(1)}, f32[192]{0:T(256)}, u32[]{:S(2)}) copy-start(f32[192]{0:T(256)} %param.25) | copy-start | bytes 2308
  163.5 47.4 %copy-start.10 = (f32[192]{0:T(256)S(1)}, f32[192]{0:T(256)}, u32[]{:S(2)}) copy-start(f32[192]{0:T(256)} %param.27) | copy-start | bytes 2308
  163.5 47.4 %copy-start.11 = (f32[192]{0:T(256)S(1)}, f32[192]{0:T(256)}, u32[]{:S(2)}) copy-start(f32[192]{0:T(256)} %param.26) | copy-start | bytes 2308
  210.9 7.0 %copy-start.8 = (bf16[768,512]{1,0:T(8,128)(2,1)S(1)}, bf16[768,512]{1,0:T(8,128)(2,1)}, u32[]{:S(2)}) copy-start(bf16[768,512]{1,0:T(8,128)(2,1)} %get-tuple-element.46) | copy-start | bytes 2359300
  212.3 6.6 %copy-start.7 = (f32[3,256,512]{2,1,0:T(8,128)S(1)}, f32[3,256,512]{2,1,0:T(8,128)}, u32[]{:S(2)}) copy-start(f32[3,256,512]{2,1,0:T(8,128)} %get-tuple-element.102) | copy-start | bytes 4718596
  218.0 2.0 copy-start.6
